TPU v7x, 32 devices: a whole 2x2x4 slice. The times are simulated.
32 devices in a mesh: grp: 4 (over y, x), slab: 8 (over z, core).
Axes of the slice: x: 2, y: 2, z: 4, core: 2. Of those that a mesh axis runs over, the one named last changes fastest.
Arguments:
- state: float32 [4, 2, 256, 128, 256], P(None, None, 'grp', 'slab'), may hold values from -5.6 to 5.6
- kz_group: int32 [256], replicated, may hold values from 0 to 7, as said below
- cutoffs: int32 [3], replicated, may hold values from 28 to 32
- damping: float32 [8], replicated, may hold values from 0.005 to 0.5
- power: float32 [8], replicated, may hold values from 0.2 to 4
Outputs:
- new_state: float32 [4, 2, 256, 128, 256], P(None, None, 'grp', 'slab')
Inputs may be any that keep to these rules, and one draw needn't show every extreme that they name: `kz_group`: each of the 8 groups holds exactly 32 indices.
All inputs are finite; a program needn't handle non-finite values.
Results may differ from a plain program's by a relative error of at most 0.00005.
Values sent between devices are 32-bit elements; how exact they have to be, the bound alone decides.
A program may use at most 192 MiB of HBM per device.

v0:
```python
import math

import jax
import jax.numpy as jnp
from jax import lax
from jax.sharding import PartitionSpec as P

PRECISE = lax.Precision.HIGH
TWO_PI = 6.283185307179586
TIME_STEP = 0.25
CORIOLIS = 1.0
BRUNT_SQUARED = 2.0
EPSILON = 1e-06


def signed(index, length):
    return jnp.where(index < length // 2, index, index - length)


def angles(modes, points, length):
    phase = modes[:, None] * points[None, :] % length
    theta = phase.astype(jnp.float32) * (TWO_PI / length)
    return (jnp.cos(theta), jnp.sin(theta))


def times_i(entries):
    return jnp.stack([-entries[1], entries[0]])


def mul(pattern, left, right):
    return jnp.einsum(pattern, left, right, precision=PRECISE)


def exchange(pieces, axis):
    shape = pieces.shape
    flat = pieces.reshape(shape[0], -1, shape[-2] * shape[-1])
    return lax.all_to_all(flat, axis, split_axis=0, concat_axis=0, tiled=True).reshape(shape)


def shards(state, kz_group, cutoffs, damping, power):
    grp_count = lax.axis_size("grp")
    slab_count = lax.axis_size("slab")
    grp_index = lax.axis_index("grp")
    slab_index = lax.axis_index("slab")
    slots_here = state.shape[2]
    cols_here = state.shape[3]
    NY = state.shape[4]
    NZ = slots_here * grp_count
    KX = cols_here * slab_count
    NX = 2 * KX
    GROUPS = damping.shape[0]
    GMODES = NZ // GROUPS
    rows_here = NY // grp_count
    planes_here = NZ // slab_count
    groups_here = GROUPS // grp_count
    normalizer = 1.0 / math.sqrt(NX * NY * NZ)
    slot_mode = jnp.argsort(kz_group, stable=True)
    local_mode = lax.dynamic_slice_in_dim(slot_mode, grp_index * slots_here, slots_here)
    mode_z = signed(local_mode, NZ)
    mode_x = slab_index * cols_here + jnp.arange(cols_here, dtype=jnp.int32)
    mode_y = signed(jnp.arange(NY, dtype=jnp.int32), NY)
    wave_z = (TWO_PI / NZ * mode_z.astype(jnp.float32))[:, None, None]
    wave_x = (TWO_PI / NX * mode_x.astype(jnp.float32))[None, :, None]
    wave_y = (TWO_PI / NY * mode_y.astype(jnp.float32))[None, None, :]
    flow_x, flow_y, flow_z, buoyant = (state[0], state[1], state[2], state[3])

    real_part = state[:, 0]
    imag_part = state[:, 1]
    cell_flux = real_part[2] * real_part[3] + imag_part[2] * imag_part[3]
    cell_energy = 0.5 * (
        jnp.sum(real_part[:3] ** 2 + imag_part[:3] ** 2, axis=0)
        + (real_part[3] ** 2 + imag_part[3] ** 2) / BRUNT_SQUARED
    )
    partial_value = jnp.stack(
        [jnp.sum(cell_flux, axis=(1, 2)), jnp.sum(cell_energy, axis=(1, 2))], axis=1
    )
    partial_value = jnp.sum(partial_value.reshape(groups_here, GMODES, 2), axis=1)
    totals = lax.psum(partial_value, "slab")
    means = totals / (GMODES * KX * NY)

    points_y = jnp.arange(NY, dtype=jnp.int32)
    points_z = jnp.arange(NZ, dtype=jnp.int32)
    points_x = jnp.arange(NX, dtype=jnp.int32)
    cosine_y, sine_y = angles(points_y, points_y, NY)
    from_real = jnp.stack([cosine_y, sine_y], axis=1)
    from_imag = jnp.stack([-sine_y, cosine_y], axis=1)
    column = wave_y.reshape(NY, 1, 1)
    shape_y = (NY, 2, grp_count, rows_here)
    spread = "fsxm,mdgy->gfdsxy"
    main = mul(spread, real_part, from_real.reshape(shape_y)) + mul(
        spread, imag_part, from_imag.reshape(shape_y)
    )
    slope = mul(spread, real_part[::2][:2], (column * from_imag).reshape(shape_y)) - mul(
        spread, imag_part[::2][:2], (column * from_real).reshape(shape_y)
    )
    pieces = exchange(jnp.concatenate([main, slope], axis=1), "grp")

    all_z = (TWO_PI / NZ * signed(slot_mode, NZ).astype(jnp.float32)).reshape(
        grp_count, slots_here, 1, 1
    )
    real_in, imag_in = (pieces[:, :, 0], pieces[:, :, 1])
    ru, rv, rw, rb, ruy, rwy = (real_in[:, k] for k in range(6))
    iu, iv, iw, ib, iuy, iwy = (imag_in[:, k] for k in range(6))
    reals = [ru, rv, rw, rb, rwy + all_z * iv, wave_x * iw - all_z * iu, -wave_x * iv - ruy]
    imags = [iu, iv, iw, ib, iwy - all_z * rv, all_z * ru - wave_x * rw, wave_x * rv - iuy]
    width = cols_here * rows_here
    reals = jnp.stack([r.reshape(NZ, width) for r in reals])
    imags = jnp.stack([r.reshape(NZ, width) for r in imags])
    cosine_z, sine_z = angles(slot_mode, points_z, NZ)
    shape_z = (NZ, 2, slab_count, planes_here)
    spread = "fsn,sdlz->lfdzn"
    grid_z = mul(spread, reals, jnp.stack([cosine_z, sine_z], axis=1).reshape(shape_z)) + mul(
        spread, imags, jnp.stack([-sine_z, cosine_z], axis=1).reshape(shape_z)
    )
    grid_z = grid_z.reshape(slab_count, 7, 2, planes_here, cols_here, rows_here)
    pieces = exchange(grid_z, "slab")

    weights = jnp.where(jnp.arange(KX) == 0, 1.0, 2.0).astype(jnp.float32) * normalizer
    cosine_x, sine_x = angles(jnp.arange(KX, dtype=jnp.int32), points_x, NX)
    shape_x = (2, slab_count, cols_here, NX)
    table_x = jnp.stack([cosine_x * weights[:, None], -sine_x * weights[:, None]]).reshape(shape_x)
    lines = pieces.transpose(1, 3, 5, 2, 0, 4).reshape(7, planes_here, rows_here, 2 * KX)
    grid = mul("fzyk,kn->fzyn", lines, table_x.reshape(2 * KX, NX))
    gu, gv, gw, gb, gox, goy, goz = (grid[k] for k in range(7))
    products = jnp.stack(
        [gv * goz - gw * goy, gw * gox - gu * goz, gu * goy - gv * gox, gu * gb, gv * gb, gw * gb]
    )
    table_b = jnp.stack([cosine_x * normalizer, -sine_x * normalizer]).reshape(2 * KX, NX)
    sectioned = mul("fzyn,kn->fzyk", products, table_b)
    sectioned = sectioned.reshape(6, planes_here, rows_here, 2, slab_count, cols_here)
    pieces = exchange(sectioned.transpose(4, 0, 3, 1, 5, 2), "slab")

    reals = pieces[:, :, 0].reshape(slab_count, 6, planes_here, width)
    imags = pieces[:, :, 1].reshape(slab_count, 6, planes_here, width)
    shape_z = (slab_count, planes_here, 2, grp_count, slots_here)
    cosine_z, sine_z = (cosine_z.T, sine_z.T)
    spread = "lfzn,lzdgs->dfgsn"
    back_z = mul(spread, reals, jnp.stack([cosine_z, -sine_z], axis=1).reshape(shape_z)) + mul(
        spread, imags, jnp.stack([sine_z, cosine_z], axis=1).reshape(shape_z)
    )
    back_z = back_z.reshape(2, 6, grp_count, slots_here, cols_here, rows_here)
    moved = wave_x * back_z[:, 3] + all_z * back_z[:, 5]
    chosen = [back_z[:, 0], back_z[:, 1], back_z[:, 2], moved, back_z[:, 4]]
    sent = jnp.stack([c.transpose(1, 0, 2, 3, 4) for c in chosen], axis=1)
    pieces = exchange(sent, "grp")

    lines = pieces.transpose(1, 2, 3, 4, 0, 5).reshape(5, 2, slots_here, cols_here, NY)
    table_r = jnp.stack([cosine_y, -sine_y], axis=1)
    table_i = jnp.stack([sine_y, cosine_y], axis=1)
    spread = "fsxy,ydm->fdsxm"
    tendency = mul(spread, lines[:, 0], table_r) + mul(spread, lines[:, 1], table_i)

    kept = (
        (96 * jnp.abs(mode_z) <= cutoffs[2] * NZ)[:, None, None]
        & (96 * mode_x <= cutoffs[0] * NX)[None, :, None]
        & (96 * jnp.abs(mode_y) <= cutoffs[1] * NY)[None, None, :]
    ).astype(jnp.float32)
    moment_x, moment_y, moment_z = (tendency[0] * kept, tendency[1] * kept, tendency[2] * kept)
    divergence = tendency[3] + wave_y * tendency[4]
    source_b = jnp.stack([divergence[1], -divergence[0]]) * kept
    power_here = lax.dynamic_slice_in_dim(power, grp_index * groups_here, groups_here)
    damping_here = lax.dynamic_slice_in_dim(damping, grp_index * groups_here, groups_here)
    forcing = (power_here - means[:, 0]) / (2.0 * (means[:, 1] + EPSILON))
    forcing_slot = jnp.repeat(forcing, GMODES)[:, None, None]
    damping_slot = jnp.repeat(damping_here, GMODES)[:, None, None]
    right_x = flow_x + TIME_STEP * (moment_x + forcing_slot * flow_x)
    right_y = flow_y + TIME_STEP * (moment_y + forcing_slot * flow_y)
    right_z = flow_z + TIME_STEP * (moment_z + forcing_slot * flow_z)
    right_b = buoyant + TIME_STEP * source_b
    wave_sq = wave_x * wave_x + wave_y * wave_y + wave_z * wave_z
    implicit = 1.0 + TIME_STEP * damping_slot * wave_sq
    rotation = TIME_STEP * CORIOLIS
    first_den = implicit * implicit + rotation * rotation
    second_den = implicit * implicit + TIME_STEP * TIME_STEP * BRUNT_SQUARED
    new_x = (implicit * right_x + rotation * right_y) / first_den
    new_y = (implicit * right_y - rotation * right_x) / first_den
    new_z = (implicit * right_z + TIME_STEP * right_b) / second_den
    new_b = (implicit * right_b - TIME_STEP * BRUNT_SQUARED * right_z) / second_den
    inverse_sq = 1.0 / (wave_sq + (wave_sq == 0).astype(jnp.float32))
    inner = (wave_x * new_x + wave_y * new_y + wave_z * new_z) * inverse_sq
    new_x = new_x - wave_x * inner
    new_y = new_y - wave_y * inner
    new_z = new_z - wave_z * inner
    return jnp.stack([new_x, new_y, new_z, new_b])


def solution(mesh):
    return jax.shard_map(
        shards,
        mesh=mesh,
        in_specs=(P(None, None, "grp", "slab", None), P(), P(), P(), P()),
        out_specs=P(None, None, "grp", "slab", None),
        check_vma=False,
    )
```

profile of v0, /device:TPU:9, one launch (start us, length us, event | category | flops | bytes accessed | tf_op | source)
XLA Modules:
  0.0 1524.7 jit_solution(4487430191423126690)
XLA Ops:
  5.6 6.7 copy_bitcast_fusion.6
  12.3 10.6 fusion.30
  23.0 15.6 %add_bitcast_fusion = f32[4,4,2,64,16,64]{3,5,4,1,0,2:T(8,128)} fusion(f32[2,4,64,4,64,16]{4,2,5,3,1,0:T(8,128)} %fusion.30, f32[4,1,64,16,256]{4,3,2,1,0:T(8,128)S(1)} %get-tuple-element.41, f32[256,1,4,64]{0,3,2,1:T(8,128)S(1)} %get-tuple-element.65, f32[256,1,4,64]{0,3,2,1:T(8,128)S(1)} %get-tuple-element.64), kind=kOutput, calls=%fused_computation.1 | convolution fusion | flops 3223453696 | bytes 21495808 | tf_op jit(solution)/shard_map/fsxm,mdgy->gfdsxy/dot_general | solution.py:31
  42.4 5.5 subtract_bitcast_fusion
  48.0 10.5 pad_maximum_fusion
  58.4 25.9 %copy.25 = f32[4,6,2,64,16,64]{5,4,3,2,1,0:T(8,128)} copy(f32[4,6,2,64,16,64]{3,5,4,1,0,2:T(8,128)} %pad_maximum_fusion) | data formatting | bytes 25165824 | tf_op jit(solution)/shard_map/concatenate | solution.py:96
  84.3 21.3 %reshape.1089 = f32[4,768,1024]{2,1,0:T(8,128)} reshape(f32[4,6,2,64,16,64]{5,4,3,2,1,0:T(8,128)} %copy.25) | data formatting | bytes 25165824 | tf_op jit(solution)/shard_map/reshape | solution.py:36
  105.7 6.6 all-to-all-start
  118.9 130.3 %all-to-all-done = f32[4,768,1024]{2,1,0:T(8,128)} async-done(((f32[4,768,1024]{2,1,0:T(8,128)}), f32[4,768,1024]{2,1,0:T(8,128)}, u32[]{:S(2)}, u32[]{:S(2)}) %all-to-all-start) | async-done | bytes 12582944 | tf_op jit(solution)/shard_map/all_to_all | solution.py:37
  249.1 19.7 %reshape.1090 = f32[4,6,2,64,16,64]{5,4,3,2,1,0:T(8,128)} reshape(f32[4,768,1024]{2,1,0:T(8,128)} %all-to-all-done) | data formatting | bytes 25165824 | tf_op jit(solution)/shard_map/reshape | solution.py:37
  268.8 18.2 %slice_bitcast_fusion.1 = (f32[4,6,64,16,64]{4,3,2,1,0:T(8,128)}, f32[4,6,64,16,64]{4,3,2,1,0:T(8,128)}) fusion(f32[4,6,2,64,16,64]{5,4,3,2,1,0:T(8,128)} %reshape.1090), kind=kLoop, calls=%fused_computation.4 | loop fusion | bytes 25165824 | tf_op jit(solution)/shard_map/squeeze | solution.py:101
  287.0 8.8 fusion.148
  304.2 9.4 fusion.149
  350.8 13.5 fusion.6
  364.3 12.4 add_bitcast_fusion.1
  376.7 13.6 copy.26
  390.4 7.1 all-to-all-start.1
  398.7 313.9 %all-to-all-done.1 = f32[8,448,1024]{2,1,0:T(8,128)} async-done(((f32[8,448,1024]{2,1,0:T(8,128)}), f32[8,448,1024]{2,1,0:T(8,128)}, u32[]{:S(2)}, u32[]{:S(2)}) %all-to-all-start.1) | async-done | bytes 14680096 | tf_op jit(solution)/shard_map/all_to_all | solution.py:37
  712.6 22.6 %reshape.1091 = f32[8,7,2,32,16,64]{5,4,3,2,1,0:T(8,128)} reshape(f32[8,448,1024]{2,1,0:T(8,128)} %all-to-all-done.1) | data formatting | bytes 29360128 | tf_op jit(solution)/shard_map/reshape | solution.py:37
  735.2 22.2 %copy.27 = f32[7,32,64,2,8,16]{2,5,4,3,1,0:T(8,128)} copy(f32[7,32,64,2,8,16]{2,5,1,3,0,4:T(8,128)} %bitcast.332) | data formatting | bytes 29360128 | tf_op jit(solution)/shard_map/transpose | solution.py:122
  757.4 31.3 %fusion.153 = f32[7,32,64,256]{3,2,1,0:T(8,128)} fusion(f32[7,32,64,256]{2,3,1,0:T(8,128)} %bitcast.331, f32[256,256,1,1]{1,0,3,2:T(8,128)S(1)} %bitcast.339), kind=kOutput, calls=%fused_computation.266 | convolution fusion | flops 5637144576 | bytes 29622272 | tf_op jit(solution)/shard_map/fzyk,kn->fzyn/dot_general | solution.py:31
  793.1 4.9 subtract_dynamic-update-slice_fusion.1
  805.4 13.1 fusion.3
  818.5 9.0 copy.29
  827.6 21.3 %reshape.1093 = f32[8,384,1024]{2,1,0:T(8,128)} reshape(f32[8,6,2,32,16,64]{5,4,3,2,1,0:T(8,128)} %copy.29) | data formatting | bytes 25165824 | tf_op jit(solution)/shard_map/reshape | solution.py:36
  848.9 9.3 all-to-all-start.2
  861.7 266.7 %all-to-all-done.2 = f32[8,384,1024]{2,1,0:T(8,128)} async-done(((f32[8,384,1024]{2,1,0:T(8,128)}), f32[8,384,1024]{2,1,0:T(8,128)}, u32[]{:S(2)}, u32[]{:S(2)}) %all-to-all-start.2) | async-done | bytes 12582944 | tf_op jit(solution)/shard_map/all_to_all | solution.py:37
  1128.4 19.7 %reshape.1094 = f32[8,6,2,32,16,64]{5,4,3,2,1,0:T(8,128)} reshape(f32[8,384,1024]{2,1,0:T(8,128)} %all-to-all-done.2) | data formatting | bytes 25165824 | tf_op jit(solution)/shard_map/reshape | solution.py:37
  1148.0 18.4 %fusion.147 = (f32[8,6,1,32,16,64]{5,4,3,2,1,0:T(8,128)}, f32[8,6,1,32,16,64]{5,4,3,2,1,0:T(8,128)}) fusion(f32[8,6,2,32,16,64]{5,4,3,2,1,0:T(8,128)} %reshape.1094), kind=kLoop, calls=%fused_computation.260 | loop fusion | bytes 25165824 | tf_op jit(solution)/shard_map/slice | solution.py:133
  1166.5 11.5 reshape.1125
  1178.0 11.6 reshape.1124
  1189.6 8.8 fusion.10
  1198.4 10.6 fusion
  1209.0 19.7 %reshape.1095 = f32[2,6,4,64,16,64]{5,4,3,1,2,0:T(8,128)} reshape(f32[2,6,4,64,1024]{4,3,1,2,0:T(8,128)} %fusion) | data formatting | bytes 25165824 | tf_op jit(solution)/shard_map/reshape | solution.py:141
  1228.6 16.4 %fusion.146 = (f32[2,1,4,64,16,64]{5,4,3,1,2,0:T(8,128)S(1)}, f32[2,1,4,64,16,64]{5,4,3,1,2,0:T(8,128)}, f32[2,1,4,64,16,64]{5,4,3,1,2,0:T(8,128)}, f32[2,1,4,64...) fusion(f32[2,6,4,64,16,64]{5,4,3,1,2,0:T(8,128)} %reshape.1095), kind=kLoop, calls=%fused_computation.259 | loop fusion | bytes 25165824 | tf_op jit(solution)/shard_map/slice | solution.py:143
  1263.9 18.2 %reshape.1096 = f32[4,640,1024]{2,1,0:T(8,128)} reshape(f32[4,5,2,64,16,64]{5,4,3,2,1,0:T(8,128)} %fusion.20) | data formatting | bytes 20971520 | tf_op jit(solution)/shard_map/reshape | solution.py:36
  1282.0 6.0 all-to-all-start.3
  1296.9 12.9 psum.7
  1320.1 7.6 fusion.150
  1327.8 74.7 %all-to-all-done.3 = f32[4,640,1024]{2,1,0:T(8,128)} async-done(((f32[4,640,1024]{2,1,0:T(8,128)}), f32[4,640,1024]{2,1,0:T(8,128)}, u32[]{:S(2)}, u32[]{:S(2)}) %all-to-all-start.3) | async-done | bytes 10485792 | tf_op jit(solution)/shard_map/all_to_all | solution.py:37
  1402.5 16.5 %reshape.1097 = f32[4,5,2,64,16,64]{5,4,3,2,1,0:T(8,128)} reshape(f32[4,640,1024]{2,1,0:T(8,128)} %all-to-all-done.3) | data formatting | bytes 20971520 | tf_op jit(solution)/shard_map/reshape | solution.py:37
  1419.0 25.5 %copy.38 = f32[5,2,64,16,4,64]{5,4,2,3,0,1:T(4,128)} copy(f32[5,2,64,16,4,64]{5,3,2,1,0,4:T(8,128)} %bitcast.333) | data formatting | bytes 20971520 | tf_op jit(solution)/shard_map/transpose | solution.py:147
  1444.5 19.8 %reshape.1098 = f32[5,2,64,16,256]{4,2,3,0,1:T(8,128)} reshape(f32[5,2,64,16,4,64]{5,4,2,3,0,1:T(4,128)} %copy.38) | data formatting | bytes 20971520 | tf_op jit(solution)/shard_map/reshape | solution.py:147
  1464.3 11.1 fusion.16
  1475.4 8.8 add_bitcast_fusion.2
  1489.0 8.0 add_divide_fusion.1
  1497.1 14.5 multiply_subtract_fusion.2
  1516.3 8.1 copy.46
  (185 shorter events, 123.5 us)
Async XLA Ops:
  0.0 42.3 %copy-start.30 = (f32[256]{0:T(256)}, f32[256]{0:T(256)S(1)}, u32[]{:S(2)}) copy-start(f32[256]{0:T(256)S(1)} %convert_multiply_fusion) | copy-start | bytes 3076
  38.6 9.3 slice-start
  38.6 9.3 slice-start.1
  42.4 5.6 slice-start.2
  42.4 5.6 slice-start.3
  105.7 7.5 copy-start.39
  105.7 143.4 %all-to-all-start = ((f32[4,768,1024]{2,1,0:T(8,128)}), f32[4,768,1024]{2,1,0:T(8,128)}, u32[]{:S(2)}, u32[]{:S(2)}) async-start(f32[4,768,1024]{2,1,0:T(8,128)} %reshape.1089), calls=%async_computation | async-start | bytes 25165824 | tf_op jit(solution)/shard_map/all_to_all | solution.py:37
  116.4 152.4 %copy-start.34 = (s32[256]{0:T(256)}, s32[256]{0:T(256)S(1)}, u32[]{:S(2)}) copy-start(s32[256]{0:T(256)S(1)} %get-tuple-element.6) | copy-start | bytes 3076
  327.5 3.2 copy-start.16
  327.5 3.2 copy-start.24
  328.5 3.3 copy-start.19
  328.5 3.3 copy-start.25
  330.7 2.6 copy-start.22
  347.5 3.3 copy-start.28
  350.8 13.5 slice-start.4
  350.8 13.5 slice-start.5
  350.8 13.5 copy-start.27
  390.4 322.3 %all-to-all-start.1 = ((f32[8,448,1024]{2,1,0:T(8,128)}), f32[8,448,1024]{2,1,0:T(8,128)}, u32[]{:S(2)}, u32[]{:S(2)}) async-start(f32[8,448,1024]{2,1,0:T(8,128)} %bitcast.336), calls=%async_computation.1 | async-start | bytes 29360128 | tf_op jit(solution)/shard_map/all_to_all | solution.py:37
  788.7 10.1 copy-start
  800.9 4.6 copy-start.7
  848.9 9.3 copy-start.35
  848.9 9.5 copy-start.33
  848.9 279.4 %all-to-all-start.2 = ((f32[8,384,1024]{2,1,0:T(8,128)}), f32[8,384,1024]{2,1,0:T(8,128)}, u32[]{:S(2)}, u32[]{:S(2)}) async-start(f32[8,384,1024]{2,1,0:T(8,128)} %reshape.1093), calls=%async_computation.2 | async-start | bytes 25165824 | tf_op jit(solution)/shard_map/all_to_all | solution.py:37
  1189.6 8.8 copy-start.2
  1245.0 4.7 copy-start.9
  1249.7 3.7 copy-start.8
  1253.4 3.7 copy-start.10
  1253.4 5.0 copy-start.11
  1253.4 5.0 copy-start.37
  1282.0 120.5 %all-to-all-start.3 = ((f32[4,640,1024]{2,1,0:T(8,128)}), f32[4,640,1024]{2,1,0:T(8,128)}, u32[]{:S(2)}, u32[]{:S(2)}) async-start(f32[4,640,1024]{2,1,0:T(8,128)} %reshape.1096), calls=%async_computation.3 | async-start | bytes 20971520 | tf_op jit(solution)/shard_map/all_to_all | solution.py:37
  1291.8 18.0 %copy-start.40 = (f32[8]{0:T(128)S(1)}, f32[8]{0:T(128)}, u32[]{:S(2)}) copy-start(f32[8]{0:T(128)} %param.9) | copy-start | bytes 100
  1291.8 18.0 %copy-start.41 = (f32[8]{0:T(128)S(1)}, f32[8]{0:T(128)}, u32[]{:S(2)}) copy-start(f32[8]{0:T(128)} %param.8) | copy-start | bytes 100
  1291.8 18.3 %copy-start.38 = (s32[3]{0:T(128)S(1)}, s32[3]{0:T(128)}, u32[]{:S(2)}) copy-start(s32[3]{0:T(128)} %param.7) | copy-start | bytes 40
  1464.3 11.1 copy-start.1
  1464.3 11.1 copy-start.26
  1464.3 11.1 copy-start.29
  1475.4 8.9 copy-start.31
  1475.4 9.5 copy-start.14
  1475.4 9.5 copy-start.15
  1484.3 3.0 copy-start.4
  1484.3 3.6 copy-start.5
  1484.3 4.2 copy-start.6
  1484.3 4.4 copy-start.12
  1484.4 4.7 copy-start.13
  1484.9 12.2 copy-start.17
  1484.9 12.2 copy-start.18
  1511.6 3.7 copy-start.20
  1511.6 4.1 copy-start.21
  (4 other events, 4.9 us)
where the time goes:
time: 1540 us; the launch traced here: 1520 us
  waiting for transfers between devices  786 us (51%)
  local copies, waits for them, and re-layouts  461 us (30%)
  matrix products  145 us (9%)
  other arithmetic  87.9 us (6%)
  starting transfers between devices  29 us (2%)
    all_to_all x4, waiting for transfers between devices, exchange(): lax.all_to_all(flat, axis, split_axis=0, concat_axis=0, tiled=True)  786 us
    dot_general x12, matrix products, mul(): return jnp.einsum(pattern, left, right, precision=PRECISE)  145 us
    reshape x4, local copies, waits for them, and re-layouts, exchange(): lax.all_to_all(flat, axis, split_axis=0, concat_axis=0, tiled=True)  78.4 us
    reshape x3, local copies, waits for them, and re-layouts, exchange(): flat = pieces.reshape(shape[0], -1, shape[-2] * shape[-1])  60.8 us
    unnamed x105, local copies, waits for them, and re-layouts  32.2 us
  transfers between devices with their start and end apart: 4, of which 4 were waited for; matrix products, arithmetic and copies ran while one was open for 2% of the time, Pallas kernels for 0%

commit v1 on v0

v1 whole, which is shorter than its diff:
```python
import functools
import math

import jax
import jax.numpy as jnp
import numpy as np
from jax import lax
from jax.experimental import pallas as pl
from jax.experimental.pallas import tpu as pltpu
from jax.sharding import PartitionSpec as P

TWO_PI = 6.283185307179586
TIME_STEP = 0.25
CORIOLIS = 1.0
BRUNT_SQUARED = 2.0
EPSILON = 1e-06
CHUNKS = 2
FIELDS = 6
RETURNS = 5


def signed(index, length):
    return jnp.where(index < length // 2, index, index - length)


def halves(values):
    high = values.astype(jnp.bfloat16)
    low = (values - high.astype(jnp.float32)).astype(jnp.bfloat16)
    return high, low


def constant_halves(table):
    table = np.asarray(table, np.float32)
    high = table.astype(jnp.bfloat16)
    low = (table - high.astype(np.float32)).astype(jnp.bfloat16)
    return jnp.asarray(high), jnp.asarray(low)


def dot3(left, right, dims=(((1,), (0,)), ((), ()))):
    dot = functools.partial(lax.dot_general, dimension_numbers=dims, preferred_element_type=jnp.float32)
    return dot(left[0], right[0]) + (dot(left[0], right[1]) + dot(left[1], right[0]))


def trig(modes, points, length):
    phase = np.asarray(modes)[:, None] * np.asarray(points)[None, :] % length
    theta = phase * (2.0 * math.pi / length)
    return np.cos(theta), np.sin(theta)


def flat_rows(ref):
    shape = ref.shape
    return ref.reshape(math.prod(shape[:-1]), shape[-1])


def strided(ref, start, count, stride):
    return ref[pl.ds(start, count, stride=stride), :]


def forward_y(cols, slots, width, *refs):
    high_ref, low_ref, out_ref = refs[width:]
    out = flat_rows(out_ref)
    lanes = 2 * slots
    count = high_ref.shape[1] // 2
    rows = [flat_rows(ref) for ref in refs[:width]]
    table = (high_ref[0], low_ref[0])
    sign = jnp.where(lax.broadcasted_iota(jnp.int32, (1, lanes), 1) < slots, -1.0, 1.0)
    pair = 2 if cols % 2 == 0 else 1
    def some(first):
        taken = []
        for j in range(pair):
            for d in range(2):
                start = d * slots * cols + first + j
                taken.append(jnp.concatenate([strided(part, start, slots, cols) for part in rows], axis=1))
        data = halves(jnp.concatenate(taken, axis=0))
        both = dot3(table, data, (((1,), (1,)), ((), ())))
        for j in range(pair):
            part = both[:, j * lanes : (j + 1) * lanes]
            result = part[:count] + sign * pltpu.roll(part[count:], slots, 1)
            out[pl.ds(first + j, count, stride=cols), :] = result

    unrolled = 2 if cols % (2 * pair) == 0 else 1

    def several(i, carry):
        for k in range(unrolled):
            some((i * unrolled + k) * pair)
        return carry

    lax.fori_loop(0, cols // (pair * unrolled), several, 0)


def planes(groups, slabs, x_step, in_ref, zf_refs, xf_refs, xb_refs, zb_refs, kz_ref, out_ref):
    cols, lanes = in_ref.shape[3:]
    kx = slabs * cols
    nz = zf_refs[0].shape[1] // 2

    def field(f):
        parts = []
        for g in range(groups):
            part = in_ref[g * slabs : (g + 1) * slabs, 0, f]
            parts.append(part.reshape(kx, lanes))
        return jnp.concatenate(parts, axis=1)

    u, u_y, w, w_y, v, b = (field(f) for f in range(FIELDS))
    wave_z = kz_ref[0:1, :]
    wave_x = x_step * lax.broadcasted_iota(jnp.int32, (kx, 1), 0).astype(jnp.float32)
    omega_x = w_y - wave_z * v
    omega_y = wave_z * u - wave_x * w
    omega_z = wave_x * v - u_y
    stacked = halves(jnp.concatenate([u, v, w, b, omega_x, omega_y, omega_z], axis=0))
    lines = dot3(stacked, (zf_refs[0][...], zf_refs[1][...]))
    grids = []
    for f in range(7):
        line = lines[f * kx : (f + 1) * kx]
        line = halves(jnp.concatenate([line[:, :nz], line[:, nz:]], axis=0))
        kind = 0 if f < 4 else 1
        grids.append(dot3((xf_refs[0][kind], xf_refs[1][kind]), line))
    gu, gv, gw, gb, gox, goy, goz = grids
    products = [gv * goz - gw * goy, gw * gox - gu * goz, gu * goy - gv * gox, gu * gb, gv * gb, gw * gb]
    table = (xb_refs[0][...], xb_refs[1][...])
    backs = []
    for product in products:
        back = dot3(table, halves(product))
        backs.append(jnp.concatenate([back[:kx], back[kx:]], axis=1))
    spectra = dot3(halves(jnp.concatenate(backs, axis=0)), (zb_refs[0][...], zb_refs[1][...]))
    hats = [spectra[f * kx : (f + 1) * kx] for f in range(6)]
    moved = wave_x * hats[3] + wave_z * hats[5]
    for f, hat in enumerate([hats[0], hats[1], hats[2], moved, hats[4]]):
        for g in range(groups):
            part = hat[:, g * lanes : (g + 1) * lanes]
            out_ref[g * slabs : (g + 1) * slabs, 0, f] = part.reshape(slabs, cols, lanes)


def finish(slots, chunks, width, *refs):
    in_refs = refs[:chunks]
    state_refs = refs[chunks : chunks + width]
    high_ref, low_ref, zrow_ref, xrow_ref, yrow_ref, out_ref = refs[chunks + width : chunks + width + 6]
    out_parts = refs[chunks + width + 6 :]
    block = out_ref.shape[3]
    ny = out_ref.shape[4]
    inputs = [flat_rows(ref) for ref in in_refs]
    state = [flat_rows(ref) for ref in state_refs]
    table = (high_ref[...], low_ref[...])
    wave_z, kept_z, forcing, damping = (zrow_ref[k] for k in range(4))
    wave_y, kept_y = yrow_ref[0:1, :], yrow_ref[1:2, :]

    def load(c, d, x):
        start = (c * 2 + d) * slots * block + x
        return jnp.concatenate([strided(part, start, slots, block) for part in state], axis=1)

    def store(c, d, x, value):
        start = (c * 2 + d) * slots * block + x
        for k in range(width):
            out_parts[k][pl.ds(start, slots, stride=block), :] = value[:, 128 * k : 128 * (k + 1)]

    def one(x, carry):
        columns = []
        for f in range(RETURNS):
            pieces = []
            for rows in inputs:
                count = rows.shape[0] // (RETURNS * block)
                pieces.append(rows[pl.ds(f * block + x, count, stride=RETURNS * block), :])
            columns.append(jnp.concatenate(pieces, axis=0).T)
        both = dot3(halves(jnp.concatenate(columns, axis=0)), table)
        tends = []
        for f in range(RETURNS):
            re = both[2 * f * slots : (2 * f + 1) * slots]
            im = both[(2 * f + 1) * slots : (2 * f + 2) * slots]
            tends.append((re[:, :ny] + im[:, ny:], im[:, :ny] - re[:, ny:]))
        wave_x = xrow_ref[0, pl.ds(x, 1), :]
        kept = (kept_z * kept_y) * xrow_ref[1, pl.ds(x, 1), :]
        kept = kept * TIME_STEP
        wave_sq = wave_x * wave_x + wave_y * wave_y + wave_z * wave_z
        implicit = 1.0 + TIME_STEP * damping * wave_sq
        rotation = TIME_STEP * CORIOLIS
        first = 1.0 / (implicit * implicit + rotation * rotation)
        second = 1.0 / (implicit * implicit + TIME_STEP * TIME_STEP * BRUNT_SQUARED)
        inverse_sq = 1.0 / (wave_sq + (wave_sq == 0).astype(jnp.float32))
        growth = 1.0 + TIME_STEP * forcing
        total = [tends[3][d] + wave_y * tends[4][d] for d in range(2)]
        source = [total[1], -total[0]]
        for d in range(2):
            right_x = growth * load(0, d, x) + kept * tends[0][d]
            right_y = growth * load(1, d, x) + kept * tends[1][d]
            right_z = growth * load(2, d, x) + kept * tends[2][d]
            right_b = load(3, d, x) + kept * source[d]
            new_x = (implicit * right_x + rotation * right_y) * first
            new_y = (implicit * right_y - rotation * right_x) * first
            new_z = (implicit * right_z + TIME_STEP * right_b) * second
            new_b = (implicit * right_b - TIME_STEP * BRUNT_SQUARED * right_z) * second
            inner = (wave_x * new_x + wave_y * new_y + wave_z * new_z) * inverse_sq
            store(0, d, x, new_x - wave_x * inner)
            store(1, d, x, new_y - wave_y * inner)
            store(2, d, x, new_z - wave_z * inner)
            store(3, d, x, new_b)
        return carry

    lax.fori_loop(0, block, one, 0)
    for k in range(width):
        for c in range(4):
            for d in range(2):
                size = slots * block
                part = out_parts[k][(c * 2 + d) * size : (c * 2 + d + 1) * size, :]
                out_ref[c, d, :, :, 128 * k : 128 * (k + 1)] = part.reshape(slots, block, 128)


def whole(array):
    return pl.BlockSpec(array.shape, lambda *_: (0,) * array.ndim)


def shards(state, kz_group, cutoffs, damping, power):
    groups = lax.axis_size("grp")
    slabs = lax.axis_size("slab")
    grp_index = lax.axis_index("grp")
    slab_index = lax.axis_index("slab")
    slots = state.shape[2]
    cols = state.shape[3]
    NY = state.shape[4]
    NZ = slots * groups
    KX = cols * slabs
    NX = 2 * KX
    GROUPS = damping.shape[0]
    GMODES = NZ // GROUPS
    devices = groups * slabs
    rows_here = NY // devices
    groups_here = GROUPS // groups
    chunks = CHUNKS if rows_here % CHUNKS == 0 else 1
    rows_chunk = rows_here // chunks
    lanes = 2 * slots
    width = NY // 128
    normalizer = 1.0 / math.sqrt(NX * NY * NZ)

    mode_y = np.fft.fftfreq(NY, 1.0 / NY).astype(np.int64)
    order_y = np.arange(NY).reshape(devices, chunks, rows_chunk).transpose(1, 0, 2).reshape(-1)
    cos_y, sin_y = trig(order_y, np.arange(NY), NY)
    wave_np = TWO_PI / NY * mode_y
    plain = np.stack([cos_y.reshape(chunks, -1, NY), sin_y.reshape(chunks, -1, NY)], axis=1)
    plain = plain.reshape(chunks, 1, -1, NY)
    y_forward = constant_halves(np.concatenate([plain, plain * wave_np], axis=1))
    y_back = constant_halves(np.concatenate([cos_y, sin_y], axis=1))
    cos_x, sin_x = trig(np.arange(NX), np.arange(KX), NX)
    weights = np.where(np.arange(KX) == 0, 1.0, 2.0)[None, :] * normalizer
    x_forward = constant_halves(
        np.stack(
            [
                np.concatenate([cos_x * weights, -sin_x * weights], axis=1),
                np.concatenate([-sin_x * weights, -cos_x * weights], axis=1),
            ]
        )
    )
    x_back = constant_halves(np.concatenate([cos_x.T, -sin_x.T], axis=0) * normalizer)

    params = pltpu.CompilerParams(vmem_limit_bytes=60 * 1024 * 1024)
    sent_shape = jax.ShapeDtypeStruct((devices, rows_chunk, FIELDS, cols, lanes), jnp.float32)
    flops = 2 * 3 * FIELDS * 2 * NY * NY * cols * lanes // chunks
    sent = []
    for c in range(chunks):
        step = pl.pallas_call(
            functools.partial(forward_y, cols, slots, width),
            grid=(FIELDS,),
            in_specs=[
                pl.BlockSpec(
                    (1, 2, slots, cols, 128),
                    lambda i, k=k: (jnp.where(i < 4, i // 2 * 2, (i - 4) * 2 + 1), 0, 0, 0, k),
                )
                for k in range(width)
            ]
            + [pl.BlockSpec((1, 2 * NY // chunks, NY), lambda i: (jnp.where(i < 4, i % 2, 0), 0, 0))] * 2,
            out_specs=pl.BlockSpec((devices, rows_chunk, 1, cols, lanes), lambda i: (0, 0, i, 0, 0)),
            out_shape=sent_shape,
            compiler_params=params,
            cost_estimate=pl.CostEstimate(flops=flops, bytes_accessed=20 << 20, transcendentals=0),
        )(*[state] * width, y_forward[0][c], y_forward[1][c])
        sent.append(step)

    slot_mode = jnp.argsort(kz_group, stable=True).astype(jnp.int32)
    phase = slot_mode[:, None] * jnp.arange(NZ, dtype=jnp.int32)[None, :] % NZ
    theta = phase.astype(jnp.float32) * (TWO_PI / NZ)
    cos_z = jnp.cos(theta).reshape(groups, 1, slots, NZ)
    sin_z = jnp.sin(theta).reshape(groups, 1, slots, NZ)
    z_real = jnp.concatenate([cos_z, -sin_z], axis=1).reshape(2 * NZ, NZ)
    z_imag = jnp.concatenate([sin_z, cos_z], axis=1).reshape(2 * NZ, NZ)
    z_table = jnp.concatenate([z_real, z_imag], axis=1)
    z_high = lax.reduce_precision(z_table, 8, 7)
    z_low = (z_table - z_high).astype(jnp.bfloat16)
    z_high = z_high.astype(jnp.bfloat16)
    z_forward = (z_high, z_low)
    z_back = (z_high.T, z_low.T)
    wave_all = TWO_PI / NZ * signed(slot_mode, NZ).astype(jnp.float32)
    wave_lanes = jnp.broadcast_to(wave_all.reshape(groups, 1, slots), (groups, 2, slots)).reshape(1, 2 * NZ)
    wave_lanes = jnp.broadcast_to(wave_lanes, (8, 2 * NZ))

    def middle(zf0, zf1, xf0, xf1, xb0, xb1, zb0, zb1, in_ref, kz_ref, out_ref):
        planes(
            groups, slabs, TWO_PI / NX, in_ref, (zf0, zf1), (xf0, xf1), (xb0, xb1), (zb0, zb1), kz_ref, out_ref
        )

    tables = [*z_forward, *x_forward, *x_back, *z_back]
    back_shape = (devices, rows_chunk, RETURNS, cols, lanes)
    flops = 2 * 3 * rows_chunk * NZ * KX * (4 * 13 * NZ + 2 * 13 * NX)
    come = []
    for c in range(chunks):
        got = lax.all_to_all(sent[c], ("grp", "slab"), 0, 0, tiled=True)
        come.append(got)
    left = []
    for c in range(chunks):
        back = pl.pallas_call(
            middle,
            grid=(rows_chunk,),
            in_specs=[whole(t) for t in tables]
            + [pl.BlockSpec((devices, 1, FIELDS, cols, lanes), lambda y: (0, y, 0, 0, 0)), whole(wave_lanes)],
            out_specs=pl.BlockSpec((devices, 1, RETURNS, cols, lanes), lambda y: (0, y, 0, 0, 0)),
            out_shape=jax.ShapeDtypeStruct(back_shape, jnp.float32),
            compiler_params=params,
            cost_estimate=pl.CostEstimate(flops=flops, bytes_accessed=22 << 20, transcendentals=0),
        )(*tables, come[c], wave_lanes)
        left.append(lax.all_to_all(back, ("grp", "slab"), 0, 0, tiled=True))

    real_part = state[:, 0]
    imag_part = state[:, 1]
    cell_flux = real_part[2] * real_part[3] + imag_part[2] * imag_part[3]
    cell_energy = 0.5 * (
        jnp.sum(real_part[:3] ** 2 + imag_part[:3] ** 2, axis=0)
        + (real_part[3] ** 2 + imag_part[3] ** 2) / BRUNT_SQUARED
    )
    partial_value = jnp.stack(
        [jnp.sum(cell_flux, axis=(1, 2)), jnp.sum(cell_energy, axis=(1, 2))], axis=1
    )
    partial_value = jnp.sum(partial_value.reshape(groups_here, GMODES, 2), axis=1)
    means = lax.psum(partial_value, "slab") / (GMODES * KX * NY)
    power_here = lax.dynamic_slice_in_dim(power, grp_index * groups_here, groups_here)
    damping_here = lax.dynamic_slice_in_dim(damping, grp_index * groups_here, groups_here)
    forcing = (power_here - means[:, 0]) / (2.0 * (means[:, 1] + EPSILON))

    local_mode = signed(lax.dynamic_slice_in_dim(slot_mode, grp_index * slots, slots), NZ)
    mode_x = slab_index * cols + jnp.arange(cols, dtype=jnp.int32)
    mode_y = signed(jnp.arange(NY, dtype=jnp.int32), NY)
    zrow = jnp.stack(
        [
            TWO_PI / NZ * local_mode.astype(jnp.float32),
            (96 * jnp.abs(local_mode) <= cutoffs[2] * NZ).astype(jnp.float32),
            jnp.repeat(forcing, GMODES),
            jnp.repeat(damping_here, GMODES),
        ]
    )
    zrow = jnp.broadcast_to(zrow[:, :, None], (4, slots, NY))
    xrow = jnp.stack(
        [
            TWO_PI / NX * mode_x.astype(jnp.float32),
            (96 * mode_x <= cutoffs[0] * NX).astype(jnp.float32),
        ]
    )
    xrow = jnp.broadcast_to(xrow[:, :, None], (2, cols, NY))
    yrow = jnp.stack(
        [
            TWO_PI / NY * mode_y.astype(jnp.float32),
            (96 * jnp.abs(mode_y) <= cutoffs[1] * NY).astype(jnp.float32),
        ]
    )
    block = 8 if cols % 8 == 0 else cols
    return pl.pallas_call(
        functools.partial(finish, slots, chunks, width),
        grid=(cols // block,),
        in_specs=[
            pl.BlockSpec((devices, rows_chunk, RETURNS, block, lanes), lambda i: (0, 0, 0, i, 0))
            for _ in range(chunks)
        ]
        + [pl.BlockSpec((4, 2, slots, block, 128), lambda i, k=k: (0, 0, 0, i, k)) for k in range(width)]
        + [
            whole(y_back[0]),
            whole(y_back[1]),
            whole(zrow),
            pl.BlockSpec((2, block, NY), lambda i: (0, i, 0)),
            whole(yrow),
        ],
        out_specs=pl.BlockSpec((4, 2, slots, block, NY), lambda i: (0, 0, 0, i, 0)),
        out_shape=jax.ShapeDtypeStruct(state.shape, jnp.float32),
        scratch_shapes=[pltpu.VMEM((8 * slots * block, 128), jnp.float32)] * width,
        compiler_params=params,
        cost_estimate=pl.CostEstimate(flops=1 << 33, bytes_accessed=28 << 20, transcendentals=0),
    )(*left, *[state] * width, *y_back, zrow, xrow, yrow)


def solution(mesh):
    return jax.shard_map(
        shards,
        mesh=mesh,
        in_specs=(P(None, None, "grp", "slab", None), P(), P(), P(), P()),
        out_specs=P(None, None, "grp", "slab", None),
        check_vma=False,
    )
```

time: 1540 us -> 584 us (0.38)
  waiting for transfers between devices: 786 us -> 315 us
  local copies, waits for them, and re-layouts: 461 us -> 6.2 us
  matrix products: 145 us -> 0 us
  Pallas kernels: 0 us -> 104 us
  blocking collectives: 12.9 us -> 111 us
  other arithmetic: 87.9 us -> 14.1 us
    all_to_all x4, waiting for transfers between devices: 786 us -> 315 us  [the longest x2 223 us: shards(): got = lax.all_to_all(sent[c], ('grp', 'slab'), 0, 0, tiled=True)]
    reshape x9 -> x2, local copies, waits for them, and re-layouts: 179 us -> 0.39 us  [the longest x1 0.2 us: shards(): z_real = jnp.concatenate([cos_z, -sin_z], axis=1).reshape(2 * NZ, NZ)]
    dot_general x12 -> x0, matrix products: 145 us -> none  [mul(): return jnp.einsum(pattern, left, right, precision=PRECISE)]
    pallas_call x0 -> x5, Pallas kernels: none -> 104 us  [the longest x2 42.3 us: shards(): pl.pallas_call(middle, grid=(rows_chunk,), in_specs=[whole(t) for t in ta...]
    psum x1, blocking collectives: 12.9 us -> 111 us  [shards(): means = lax.psum(partial_value, 'slab') / (GMODES * KX * NY)]
    slice x7 -> x1, local copies, waits for them, and re-layouts: 65.6 us -> 0.67 us  [shards(): cutoffs[1] * NY]
    transpose x3 -> x0, local copies, waits for them, and re-layouts: 56.7 us -> none  [the longest x1 25.5 us: shards(): pieces.transpose(1, 2, 3, 4, 0, 5).reshape(5, 2, slots_here, cols_here, NY)]
    another operation x9 -> x2, local copies, waits for them, and re-layouts: 44 us -> 0.17 us  [shards(): jnp.stack([TWO_PI / NZ * local_mode.astype(jnp.float32), (96 * jnp.abs(lo...]
  transfers between devices with their start and end apart: 4 -> 4, of which waited for: 4 -> 3; matrix products, arithmetic and copies ran while one was open for 2% -> 3% of each run, Pallas kernels for 0% -> 10%
where the time goes in v1:
time: 584 us; the launch traced here: 583 us
  waiting for transfers between devices  315 us (54%)
  blocking collectives  111 us (19%)
  Pallas kernels  104 us (18%)
  starting transfers between devices  30.9 us (5%)
  other arithmetic  14.1 us (2%)
  local copies, waits for them, and re-layouts  6.2 us (1%)
    all_to_all x2, waiting for transfers between devices, shards(): got = lax.all_to_all(sent[c], ('grp', 'slab'), 0, 0, tiled=True)  223 us
    psum x1, blocking collectives, shards(): means = lax.psum(partial_value, 'slab') / (GMODES * KX * NY)  111 us
    all_to_all x2, waiting for transfers between devices, shards(): left.append(lax.all_to_all(back, ('grp', 'slab'), 0, 0, tiled=True))  91.6 us
    pallas_call x2, Pallas kernels, shards(): pl.pallas_call(middle, grid=(rows_chunk,), in_specs=[whole(t) for t in ta...  42.3 us
    pallas_call x2, Pallas kernels, shards(): pl.pallas_call(functools.partial(forward_y, cols, slots, width), grid=(FI...  36.7 us
    pallas_call x1, Pallas kernels, shards(): pl.pallas_call(functools.partial(finish, slots, chunks, width), grid=(col...  24.6 us
    all_to_all x2, starting transfers between devices, shards(): left.append(lax.all_to_all(back, ('grp', 'slab'), 0, 0, tiled=True))  16.4 us
    all_to_all x2, starting transfers between devices, shards(): got = lax.all_to_all(sent[c], ('grp', 'slab'), 0, 0, tiled=True)  14.5 us
  transfers between devices with their start and end apart: 4, of which 3 were waited for; matrix products, arithmetic and copies ran while one was open for 3% of the time, Pallas kernels for 10%

profile of v1, /device:TPU:9, one launch (start us, length us, event | category | flops | bytes accessed | tf_op | source)
XLA Modules:
  0.0 582.9 jit_solution(12492670089184924751)
XLA Ops:
  0.0 18.4 %shard_map.129 = f32[32,4,6,16,128]{4,3,2,1,0:T(8,128)} custom-call(f32[4,2,64,16,256]{4,3,2,1,0:T(8,128)} %refs_3_.1, f32[4,2,64,16,256]{4,3,2,1,0:T(8,128)} %refs_3_.1, bf16[2,256,256]{2,1,0:T(8,128)(2,1)} %constant.96.refs_2_, bf16[2,256,256]{2,1,0:T(8,128)(2,1)} %constant.98.refs_3_), custom_call_target="tpu_custom_call" | custom-call | flops 4831838208 | bytes 20971520 | tf_op jit(solution)/shard_map/pallas_call | solution.py:257
  18.4 6.4 %all-to-all-start.2 = ((f32[32,4,6,16,128]{4,3,2,1,0:T(8,128)}), f32[32,4,6,16,128]{4,3,2,1,0:T(8,128)}, u32[]{:S(2)}, u32[]{:S(2)}) async-start(f32[32,4,6,16,128]{4,3,2,1,0:T(8,128)} %shard_map.129), calls=%async_computation.2 | async-start | bytes 12582912 | tf_op jit(solution)/shard_map/all_to_all | solution.py:302
  24.8 18.3 %shard_map.127 = f32[32,4,6,16,128]{4,3,2,1,0:T(8,128)} custom-call(f32[4,2,64,16,256]{4,3,2,1,0:T(8,128)} %refs_3_.1, f32[4,2,64,16,256]{4,3,2,1,0:T(8,128)} %refs_3_.1, bf16[2,256,256]{2,1,0:T(8,128)(2,1)} %constant.92.refs_2_, bf16[2,256,256]{2,1,0:T(8,128)(2,1)} %constant.94.refs_3_), custom_call_target="tpu_custom_call" | custom-call | flops 4831838208 | bytes 20971520 | tf_op jit(solution)/shard_map/pallas_call | solution.py:257
  43.1 117.0 %all-to-all-done.2.in_ref = f32[32,4,6,16,128]{4,3,2,1,0:T(8,128)} async-done(((f32[32,4,6,16,128]{4,3,2,1,0:T(8,128)}), f32[32,4,6,16,128]{4,3,2,1,0:T(8,128)}, u32[]{:S(2)}, u32[]{:S(2)}) %all-to-all-start.2) | async-done | bytes 6291488 | tf_op jit(solution)/shard_map/all_to_all | solution.py:302
  160.1 8.1 %all-to-all-start = ((f32[32,4,6,16,128]{4,3,2,1,0:T(8,128)}), f32[32,4,6,16,128]{4,3,2,1,0:T(8,128)}, u32[]{:S(2)}, u32[]{:S(2)}) async-start(f32[32,4,6,16,128]{4,3,2,1,0:T(8,128)} %shard_map.127), calls=%async_computation | async-start | bytes 12582912 | tf_op jit(solution)/shard_map/all_to_all | solution.py:302
  168.2 3.2 sort.17
  171.4 0.1 mul.157
  171.5 1.1 fusion.11
  172.6 0.1 pad_maximum_fusion.1
  172.7 0.2 copy.18
  172.9 0.2 copy.19
  173.1 0.2 fusion
  173.3 0.0 copy-start
  173.3 1.2 copy.20.zf0
  174.5 1.0 copy.21.zf1
  175.5 0.1 broadcast_in_dim.16
  175.6 0.1 broadcast_in_dim.36
  175.7 0.6 broadcast_in_dim.37.kz_ref
  176.3 21.2 %shard_map.130 = f32[32,4,5,16,128]{4,3,2,1,0:T(8,128)} custom-call(bf16[512,512]{1,0:T(8,128)(2,1)} %copy.20.zf0, bf16[512,512]{1,0:T(8,128)(2,1)} %copy.21.zf1, bf16[2,256,256]{2,1,0:T(8,128)(2,1)} %constant.87.clone.xf0, bf16[2,256,256]{2,1,0:T(8,128)(2,1)} %constant.88.clone.xf1, bf16[256,256]{1,0:T(8,128)(2,1)} %constant.89.clone.xb0, ...), custom_call_target="tpu_custom_call" | custom-call | flops 15703474176 | bytes 23068672 | tf_op jit(solution)/shard_map/pallas_call | solution.py:306
  197.5 105.9 %all-to-all-done.in_ref = f32[32,4,6,16,128]{4,3,2,1,0:T(8,128)} async-done(((f32[32,4,6,16,128]{4,3,2,1,0:T(8,128)}), f32[32,4,6,16,128]{4,3,2,1,0:T(8,128)}, u32[]{:S(2)}, u32[]{:S(2)}) %all-to-all-start) | async-done | bytes 6291488 | tf_op jit(solution)/shard_map/all_to_all | solution.py:302
  303.4 8.2 %all-to-all-start.3 = ((f32[32,4,5,16,128]{4,3,2,1,0:T(8,128)}), f32[32,4,5,16,128]{4,3,2,1,0:T(8,128)}, u32[]{:S(2)}, u32[]{:S(2)}) async-start(f32[32,4,5,16,128]{4,3,2,1,0:T(8,128)} %shard_map.130), calls=%async_computation.3 | async-start | bytes 10485760 | tf_op jit(solution)/shard_map/all_to_all | solution.py:316
  311.6 21.1 %shard_map.128 = f32[32,4,5,16,128]{4,3,2,1,0:T(8,128)} custom-call(bf16[512,512]{1,0:T(8,128)(2,1)} %copy.20.zf0, bf16[512,512]{1,0:T(8,128)(2,1)} %copy.21.zf1, bf16[2,256,256]{2,1,0:T(8,128)(2,1)} %constant.87.clone.xf0, bf16[2,256,256]{2,1,0:T(8,128)(2,1)} %constant.88.clone.xf1, bf16[256,256]{1,0:T(8,128)(2,1)} %constant.89.clone.xb0, ...), custom_call_target="tpu_custom_call" | custom-call | flops 15703474176 | bytes 23068672 | tf_op jit(solution)/shard_map/pallas_call | solution.py:306
  332.8 91.6 %all-to-all-done.3.refs_1_ = f32[32,4,5,16,128]{4,3,2,1,0:T(8,128)} async-done(((f32[32,4,5,16,128]{4,3,2,1,0:T(8,128)}), f32[32,4,5,16,128]{4,3,2,1,0:T(8,128)}, u32[]{:S(2)}, u32[]{:S(2)}) %all-to-all-start.3) | async-done | bytes 5242912 | tf_op jit(solution)/shard_map/all_to_all | solution.py:316
  424.4 8.2 %all-to-all-start.1 = ((f32[32,4,5,16,128]{4,3,2,1,0:T(8,128)}), f32[32,4,5,16,128]{4,3,2,1,0:T(8,128)}, u32[]{:S(2)}, u32[]{:S(2)}) async-start(f32[32,4,5,16,128]{4,3,2,1,0:T(8,128)} %shard_map.128), calls=%async_computation.1 | async-start | bytes 10485760 | tf_op jit(solution)/shard_map/all_to_all | solution.py:316
  432.6 0.0 copy-start.4
  432.6 0.0 copy-start.5
  432.6 0.0 copy-start.2
  432.6 3.8 add_reduce_fusion
  436.4 2.1 fusion.2
  438.5 0.1 stack.35
  438.6 2.7 add_reduce_fusion.1
  441.4 0.1 stack.34
  441.4 0.1 maximum_reduce_fusion
  441.5 111.4 %psum.7 = f32[2,2]{0,1:T(2,128)S(1)} all-reduce(f32[2,2]{0,1:T(2,128)S(1)} %maximum_reduce_fusion), channel_id=1, replica_groups=mesh['grp'=4,'slab'=8] {'slab'}, use_global_device_ids=true, to_apply=%region_5.6 | all-reduce | flops 4 | bytes 32 | tf_op jit(solution)/shard_map/psum | solution.py:329
  552.9 0.1 bitcast_divide_fusion
  553.0 0.1 broadcast_in_dim.38
  553.1 0.1 stack_reshape.6
  553.2 0.1 dynamic_slice.11
  553.3 0.1 broadcast_in_dim.39
  553.3 0.1 stack_reshape.7
  553.4 0.7 fusion.15
  556.0 0.1 multiply_bitcast_fusion
  556.1 0.1 fusion.14
  556.2 0.6 pad_maximum_fusion.4.refs_8_
  556.8 0.0 all-to-all-done.1.refs_0_
  556.8 0.8 broadcast_in_dim.40.refs_6_
  557.6 0.7 broadcast_in_dim.41.refs_7_
  558.3 24.6 %shard_map.131 = f32[4,2,64,16,256]{4,3,2,1,0:T(8,128)} custom-call(f32[32,4,5,16,128]{4,3,2,1,0:T(8,128)} %all-to-all-done.1.refs_0_, f32[32,4,5,16,128]{4,3,2,1,0:T(8,128)} %all-to-all-done.3.refs_1_, f32[4,2,64,16,256]{4,3,2,1,0:T(8,128)} %refs_3_.1, f32[4,2,64,16,256]{4,3,2,1,0:T(8,128)} %refs_3_.1, bf16[256,512]{1,0:T(8,128)(2,1)} %constant.85.clone.refs_4_, ...), custom_call_target="tpu_custom_call" | custom-call | flops 8589934592 | bytes 29360128 | tf_op jit(solution)/shard_map/pallas_call | solution.py:360
  (18 shorter events, 0.1 us)
Async XLA Ops:
  18.4 141.7 %all-to-all-start.2 = ((f32[32,4,6,16,128]{4,3,2,1,0:T(8,128)}), f32[32,4,6,16,128]{4,3,2,1,0:T(8,128)}, u32[]{:S(2)}, u32[]{:S(2)}) async-start(f32[32,4,6,16,128]{4,3,2,1,0:T(8,128)} %shard_map.129), calls=%async_computation.2 | async-start | bytes 12582912 | tf_op jit(solution)/shard_map/all_to_all | solution.py:302
  43.1 125.1 %copy-start.3 = (s32[256]{0:T(256)S(1)}, s32[256]{0:T(256)}, u32[]{:S(2)}) copy-start(s32[256]{0:T(256)} %param.14) | copy-start | bytes 3076
  160.1 143.3 %all-to-all-start = ((f32[32,4,6,16,128]{4,3,2,1,0:T(8,128)}), f32[32,4,6,16,128]{4,3,2,1,0:T(8,128)}, u32[]{:S(2)}, u32[]{:S(2)}) async-start(f32[32,4,6,16,128]{4,3,2,1,0:T(8,128)} %shard_map.127), calls=%async_computation | async-start | bytes 12582912 | tf_op jit(solution)/shard_map/all_to_all | solution.py:302
  173.3 3.0 copy-start
  173.3 3.0 copy-start.1
  303.4 121.0 %all-to-all-start.3 = ((f32[32,4,5,16,128]{4,3,2,1,0:T(8,128)}), f32[32,4,5,16,128]{4,3,2,1,0:T(8,128)}, u32[]{:S(2)}, u32[]{:S(2)}) async-start(f32[32,4,5,16,128]{4,3,2,1,0:T(8,128)} %shard_map.130), calls=%async_computation.3 | async-start | bytes 10485760 | tf_op jit(solution)/shard_map/all_to_all | solution.py:316
  424.4 132.4 %all-to-all-start.1 = ((f32[32,4,5,16,128]{4,3,2,1,0:T(8,128)}), f32[32,4,5,16,128]{4,3,2,1,0:T(8,128)}, u32[]{:S(2)}, u32[]{:S(2)}) async-start(f32[32,4,5,16,128]{4,3,2,1,0:T(8,128)} %shard_map.128), calls=%async_computation.1 | async-start | bytes 10485760 | tf_op jit(solution)/shard_map/all_to_all | solution.py:316
  432.6 120.3 %copy-start.4 = (f32[8]{0:T(128)S(1)}, f32[8]{0:T(128)}, u32[]{:S(2)}) copy-start(f32[8]{0:T(128)} %param.17) | copy-start | bytes 100
  432.6 120.6 %copy-start.5 = (f32[8]{0:T(128)S(1)}, f32[8]{0:T(128)}, u32[]{:S(2)}) copy-start(f32[8]{0:T(128)} %param.16) | copy-start | bytes 100
  432.6 120.8 %copy-start.2 = (s32[3]{0:T(128)S(1)}, s32[3]{0:T(128)}, u32[]{:S(2)}) copy-start(s32[3]{0:T(128)} %param.15) | copy-start | bytes 40

commit v2 on v1

--- a/solution.py
+++ b/solution.py
@@ -14,7 +14,9 @@
 CORIOLIS = 1.0
 BRUNT_SQUARED = 2.0
 EPSILON = 1e-06
-CHUNKS = 2
+AHEAD = 3
+LAG = 3
+WIDEST = 32
 FIELDS = 6
 RETURNS = 5
 
@@ -56,8 +58,9 @@
     return ref[pl.ds(start, count, stride=stride), :]
 
 
-def forward_y(cols, slots, width, *refs):
-    high_ref, low_ref, out_ref = refs[width:]
+def forward_y(cols, slots, width, members, *refs):
+    flow_w = [flat_rows(ref) for ref in refs[width : 2 * width]]
+    high_ref, low_ref, out_ref, sums_ref = refs[2 * width :]
     out = flat_rows(out_ref)
     lanes = 2 * slots
     count = high_ref.shape[1] // 2
@@ -87,21 +90,38 @@
 
     lax.fori_loop(0, cols // (pair * unrolled), several, 0)
 
-
-def planes(groups, slabs, x_step, in_ref, zf_refs, xf_refs, xb_refs, zb_refs, kz_ref, out_ref):
-    cols, lanes = in_ref.shape[3:]
-    kx = slabs * cols
+    step = pl.program_id(0)
+    here = sums_ref.shape[0] // 2
+    size = members * cols
+
+    @pl.when(step == 0)
+    def _():
+        sums_ref[...] = jnp.zeros_like(sums_ref)
+
+    def add_up(which, one, two, weight):
+        for group in range(here):
+            for d in range(2):
+                start = (d * slots + group * members) * cols
+                for a, b in zip(one, two):
+                    product = a[pl.ds(start, size), :] * b[pl.ds(start, size), :]
+                    total = jnp.sum(product.reshape(size // 8, 8, 128), axis=0)
+                    sums_ref[which * here + group] += weight * total
+
+    @pl.when((step == 0) | (step == 2) | (step == 4))
+    def _():
+        add_up(1, rows, rows, 0.5)
+
+    @pl.when(step == 5)
+    def _():
+        add_up(1, rows, rows, 0.5 / BRUNT_SQUARED)
+        add_up(0, rows, flow_w, 1.0)
+
+
+def planes(groups, slabs, x_step, read, zf_refs, xf_refs, xb_refs, zb_refs, kz_ref, kept_ref, write):
+    wave_z = kz_ref[0:1, :]
     nz = zf_refs[0].shape[1] // 2
-
-    def field(f):
-        parts = []
-        for g in range(groups):
-            part = in_ref[g * slabs : (g + 1) * slabs, 0, f]
-            parts.append(part.reshape(kx, lanes))
-        return jnp.concatenate(parts, axis=1)
-
-    u, u_y, w, w_y, v, b = (field(f) for f in range(FIELDS))
-    wave_z = kz_ref[0:1, :]
+    u, u_y, w, w_y, v, b = (jnp.concatenate([read(g, f) for g in range(groups)], axis=1) for f in range(FIELDS))
+    kx = u.shape[0]
     wave_x = x_step * lax.broadcasted_iota(jnp.int32, (kx, 1), 0).astype(jnp.float32)
     omega_x = w_y - wave_z * v
     omega_y = wave_z * u - wave_x * w
@@ -123,11 +143,139 @@
         backs.append(jnp.concatenate([back[:kx], back[kx:]], axis=1))
     spectra = dot3(halves(jnp.concatenate(backs, axis=0)), (zb_refs[0][...], zb_refs[1][...]))
     hats = [spectra[f * kx : (f + 1) * kx] for f in range(6)]
-    moved = wave_x * hats[3] + wave_z * hats[5]
+    moved = wave_x * hats[3] + kept_ref[0:1, :] * hats[5]
     for f, hat in enumerate([hats[0], hats[1], hats[2], moved, hats[4]]):
-        for g in range(groups):
-            part = hat[:, g * lanes : (g + 1) * lanes]
-            out_ref[g * slabs : (g + 1) * slabs, 0, f] = part.reshape(slabs, cols, lanes)
+        write(f, hat)
+
+
+def travel(groups, slabs, x_step, *refs):
+    (sent, zf0, zf1, xf0, xf1, xb0, xb1, zb0, zb1, choose, kz_ref, kept_ref, sums_ref, final, totals) = refs[:15]
+    (taken, made, kept, ready, f_send, f_recv, f_own, b_send, b_recv, c_send, c_recv, c_own, t_send, t_recv, t_own) = refs[15:]
+    devices = groups * slabs
+    count = taken.shape[0]
+    cols, lanes = taken.shape[3:]
+    ahead = min(AHEAD, count)
+    lag = min(LAG, count)
+    g = lax.axis_index("grp")
+    s = lax.axis_index("slab")
+    me = g * slabs + s
+
+    def remote(source, target, send, recv, to_g, to_s):
+        pltpu.make_async_remote_copy(
+            src_ref=source,
+            dst_ref=target,
+            send_sem=send,
+            recv_sem=recv,
+            device_id={"grp": to_g, "slab": to_s},
+            device_id_type=pl.DeviceIdType.MESH,
+        ).start()
+
+    def wait_all(ref, sem):
+        pltpu.make_async_copy(ref, ref, sem).wait()
+
+    def own_f(y):
+        return pltpu.make_async_copy(sent.at[me, y], taken.at[y, me], f_own.at[y])
+
+    def send_f(y):
+        own_f(y).start()
+
+        def one(k, carry):
+            to = lax.rem(me + k, devices)
+            remote(sent.at[to, y], taken.at[y, me], f_send.at[y], f_recv.at[y], to // slabs, lax.rem(to, slabs))
+            return carry
+
+        lax.fori_loop(1, devices, one, 0)
+
+    def send_b(y):
+        def one(k, carry):
+            to = lax.rem(s + k, slabs)
+            remote(made.at[y, to], kept.at[y, s], b_send.at[y], b_recv.at[y], g, to)
+            return carry
+
+        lax.fori_loop(1, slabs, one, 0)
+
+    def own_c(y):
+        return pltpu.make_async_copy(ready.at[y, g], final.at[g, y], c_own.at[y])
+
+    def send_c(y):
+        own_c(y).start()
+        for k in range(1, groups):
+            to = lax.rem(g + k, groups)
+            remote(ready.at[y, to], final.at[g, y], c_send.at[y], c_recv.at[y], to, s)
+
+    own_t = pltpu.make_async_copy(sums_ref, totals.at[s], t_own)
+
+    def first(y, carry):
+        send_f(y)
+        return carry
+
+    lax.fori_loop(0, ahead, first, 0)
+    own_t.start()
+
+    def send_t(k, carry):
+        remote(sums_ref, totals.at[s], t_send, t_recv, g, lax.rem(s + k, slabs))
+        return carry
+
+    lax.fori_loop(1, slabs, send_t, 0)
+
+    def step(t, carry):
+        @pl.when(t < count)
+        def _():
+            own_f(t).wait()
+            wait_all(taken.at[t, pl.ds(0, devices - 1)], f_recv.at[t])
+
+            @pl.when(t + ahead < count)
+            def _():
+                send_f(t + ahead)
+
+            def read(group, f):
+                part = taken[t, group * slabs : (group + 1) * slabs, f]
+                return part.reshape(slabs * cols, lanes)
+
+            def write(f, value):
+                made[t, :, f] = value.reshape(slabs, cols, value.shape[1])
+
+            planes(
+                groups, slabs, x_step, read, (zf0, zf1), (xf0, xf1), (xb0, xb1), (zb0, zb1), kz_ref, kept_ref, write
+            )
+            kept[t, s] = made[t, s]
+
+        @pl.when(t >= lag)
+        def _():
+            y = t - lag
+            wait_all(kept.at[y, pl.ds(0, slabs - 1)], b_recv.at[y])
+            data = kept[y]
+            high, low = halves(data.reshape(slabs * RETURNS * cols, data.shape[-1]))
+            dot = functools.partial(jnp.dot, preferred_element_type=jnp.float32)
+            picked = dot(high, choose[...]) + dot(low, choose[...])
+            for group in range(groups):
+                part = picked[:, group * lanes : (group + 1) * lanes]
+                ready[y, group] = part.reshape(slabs, RETURNS, cols, lanes)
+
+        @pl.when(t < count)
+        def _():
+            send_b(t)
+
+        @pl.when(t >= lag)
+        def _():
+            send_c(t - lag)
+
+        return carry
+
+    lax.fori_loop(0, count + lag, step, 0)
+
+    def last(y, carry):
+        own_c(y).wait()
+        wait_all(final.at[pl.ds(0, groups - 1), y], c_recv.at[y])
+        wait_all(taken.at[y, pl.ds(0, devices - 1)], f_send.at[y])
+        wait_all(kept.at[y, pl.ds(0, slabs - 1)], b_send.at[y])
+        wait_all(ready.at[y, pl.ds(0, groups - 1)], c_send.at[y])
+        return carry
+
+    lax.fori_loop(0, count, last, 0)
+    own_t.wait()
+    wait_all(totals.at[pl.ds(0, slabs - 1)], t_recv)
+    wait_all(totals.at[pl.ds(0, slabs - 1)], t_send)
 
 
 def finish(slots, chunks, width, *refs):
@@ -223,20 +371,29 @@
     devices = groups * slabs
     rows_here = NY // devices
     groups_here = GROUPS // groups
-    chunks = CHUNKS if rows_here % CHUNKS == 0 else 1
-    rows_chunk = rows_here // chunks
     lanes = 2 * slots
     width = NY // 128
     normalizer = 1.0 / math.sqrt(NX * NY * NZ)
 
     mode_y = np.fft.fftfreq(NY, 1.0 / NY).astype(np.int64)
-    order_y = np.arange(NY).reshape(devices, chunks, rows_chunk).transpose(1, 0, 2).reshape(-1)
-    cos_y, sin_y = trig(order_y, np.arange(NY), NY)
+    cos_y, sin_y = trig(np.arange(NY), np.arange(NY), NY)
     wave_np = TWO_PI / NY * mode_y
-    plain = np.stack([cos_y.reshape(chunks, -1, NY), sin_y.reshape(chunks, -1, NY)], axis=1)
-    plain = plain.reshape(chunks, 1, -1, NY)
-    y_forward = constant_halves(np.concatenate([plain, plain * wave_np], axis=1))
-    y_back = constant_halves(np.concatenate([cos_y, sin_y], axis=1))
+    plain = np.concatenate([cos_y, sin_y], axis=0)
+    y_forward = constant_halves(np.stack([plain, plain * wave_np]))
+    order = np.arange(NY).reshape(groups, slabs, rows_here).transpose(0, 2, 1).reshape(-1)
+    y_back = constant_halves(np.concatenate([cos_y, sin_y], axis=1)[order])
+    reach = WIDEST * NZ // 96
+    half = -(-(2 * reach + 1) // 64) * 64
+    mode_kept = np.arange(half) - reach
+    inside = mode_kept <= reach
+    cos_k, sin_k = (part * inside for part in trig(np.arange(NZ), mode_kept, NZ))
+    z_back = constant_halves(
+        np.concatenate(
+            [np.concatenate([cos_k, -sin_k], axis=1), np.concatenate([sin_k, cos_k], axis=1)], axis=0
+        )
+    )
+    wave_kept = np.concatenate([TWO_PI / NZ * mode_kept * inside] * 2)
+    wave_kept = jnp.asarray(np.broadcast_to(wave_kept, (8, 2 * half)), jnp.float32)
     cos_x, sin_x = trig(np.arange(NX), np.arange(KX), NX)
     weights = np.where(np.arange(KX) == 0, 1.0, 2.0)[None, :] * normalizer
     x_forward = constant_halves(
@@ -250,27 +407,33 @@
     x_back = constant_halves(np.concatenate([cos_x.T, -sin_x.T], axis=0) * normalizer)
 
     params = pltpu.CompilerParams(vmem_limit_bytes=60 * 1024 * 1024)
-    sent_shape = jax.ShapeDtypeStruct((devices, rows_chunk, FIELDS, cols, lanes), jnp.float32)
-    flops = 2 * 3 * FIELDS * 2 * NY * NY * cols * lanes // chunks
-    sent = []
-    for c in range(chunks):
-        step = pl.pallas_call(
-            functools.partial(forward_y, cols, slots, width),
-            grid=(FIELDS,),
-            in_specs=[
-                pl.BlockSpec(
-                    (1, 2, slots, cols, 128),
-                    lambda i, k=k: (jnp.where(i < 4, i // 2 * 2, (i - 4) * 2 + 1), 0, 0, 0, k),
-                )
-                for k in range(width)
-            ]
-            + [pl.BlockSpec((1, 2 * NY // chunks, NY), lambda i: (jnp.where(i < 4, i % 2, 0), 0, 0))] * 2,
-            out_specs=pl.BlockSpec((devices, rows_chunk, 1, cols, lanes), lambda i: (0, 0, i, 0, 0)),
-            out_shape=sent_shape,
-            compiler_params=params,
-            cost_estimate=pl.CostEstimate(flops=flops, bytes_accessed=20 << 20, transcendentals=0),
-        )(*[state] * width, y_forward[0][c], y_forward[1][c])
-        sent.append(step)
+    state_step = [
+        pl.BlockSpec(
+            (1, 2, slots, cols, 128),
+            lambda i, k=k: (jnp.where(i < 4, i // 2 * 2, (i - 4) * 2 + 1), 0, 0, 0, k),
+        )
+        for k in range(width)
+    ]
+    state_w = [pl.BlockSpec((1, 2, slots, cols, 128), lambda i, k=k: (2, 0, 0, 0, k)) for k in range(width)]
+    sent, sums = pl.pallas_call(
+        functools.partial(forward_y, cols, slots, width, GMODES),
+        grid=(FIELDS,),
+        in_specs=state_step
+        + state_w
+        + [pl.BlockSpec((1, 2 * NY, NY), lambda i: (jnp.where(i < 4, i % 2, 0), 0, 0))] * 2,
+        out_specs=[
+            pl.BlockSpec((devices, rows_here, 1, cols, lanes), lambda i: (0, 0, i, 0, 0)),
+            pl.BlockSpec((2 * groups_here, 8, 128), lambda i: (0, 0, 0)),
+        ],
+        out_shape=[
+            jax.ShapeDtypeStruct((devices, rows_here, FIELDS, cols, lanes), jnp.float32),
+            jax.ShapeDtypeStruct((2 * groups_here, 8, 128), jnp.float32),
+        ],
+        compiler_params=params,
+        cost_estimate=pl.CostEstimate(
+            flops=2 * 3 * FIELDS * 2 * NY * NY * cols * lanes, bytes_accessed=20 << 20, transcendentals=0
+        ),
+    )(*[state] * (2 * width), *y_forward)
 
     slot_mode = jnp.argsort(kz_group, stable=True).astype(jnp.int32)
     phase = slot_mode[:, None] * jnp.arange(NZ, dtype=jnp.int32)[None, :] % NZ
@@ -284,49 +447,40 @@
     z_low = (z_table - z_high).astype(jnp.bfloat16)
     z_high = z_high.astype(jnp.bfloat16)
     z_forward = (z_high, z_low)
-    z_back = (z_high.T, z_low.T)
-    wave_all = TWO_PI / NZ * signed(slot_mode, NZ).astype(jnp.float32)
+    wave_slot = signed(slot_mode, NZ)
+    wave_all = TWO_PI / NZ * wave_slot.astype(jnp.float32)
     wave_lanes = jnp.broadcast_to(wave_all.reshape(groups, 1, slots), (groups, 2, slots)).reshape(1, 2 * NZ)
     wave_lanes = jnp.broadcast_to(wave_lanes, (8, 2 * NZ))
 
-    def middle(zf0, zf1, xf0, xf1, xb0, xb1, zb0, zb1, in_ref, kz_ref, out_ref):
-        planes(
-            groups, slabs, TWO_PI / NX, in_ref, (zf0, zf1), (xf0, xf1), (xb0, xb1), (zb0, zb1), kz_ref, out_ref
-        )
-
-    tables = [*z_forward, *x_forward, *x_back, *z_back]
-    back_shape = (devices, rows_chunk, RETURNS, cols, lanes)
-    flops = 2 * 3 * rows_chunk * NZ * KX * (4 * 13 * NZ + 2 * 13 * NX)
-    come = []
-    for c in range(chunks):
-        got = lax.all_to_all(sent[c], ("grp", "slab"), 0, 0, tiled=True)
-        come.append(got)
-    left = []
-    for c in range(chunks):
-        back = pl.pallas_call(
-            middle,
-            grid=(rows_chunk,),
-            in_specs=[whole(t) for t in tables]
-            + [pl.BlockSpec((devices, 1, FIELDS, cols, lanes), lambda y: (0, y, 0, 0, 0)), whole(wave_lanes)],
-            out_specs=pl.BlockSpec((devices, 1, RETURNS, cols, lanes), lambda y: (0, y, 0, 0, 0)),
-            out_shape=jax.ShapeDtypeStruct(back_shape, jnp.float32),
-            compiler_params=params,
-            cost_estimate=pl.CostEstimate(flops=flops, bytes_accessed=22 << 20, transcendentals=0),
-        )(*tables, come[c], wave_lanes)
-        left.append(lax.all_to_all(back, ("grp", "slab"), 0, 0, tiled=True))
-
-    real_part = state[:, 0]
-    imag_part = state[:, 1]
-    cell_flux = real_part[2] * real_part[3] + imag_part[2] * imag_part[3]
-    cell_energy = 0.5 * (
-        jnp.sum(real_part[:3] ** 2 + imag_part[:3] ** 2, axis=0)
-        + (real_part[3] ** 2 + imag_part[3] ** 2) / BRUNT_SQUARED
-    )
-    partial_value = jnp.stack(
-        [jnp.sum(cell_flux, axis=(1, 2)), jnp.sum(cell_energy, axis=(1, 2))], axis=1
-    )
-    partial_value = jnp.sum(partial_value.reshape(groups_here, GMODES, 2), axis=1)
-    means = lax.psum(partial_value, "slab") / (GMODES * KX * NY)
+    place = wave_slot + reach
+    choose = (place[None, :] == jnp.arange(half, dtype=jnp.int32)[:, None]).reshape(half, groups, 1, slots)
+    nothing = jnp.zeros_like(choose)
+    choose = jnp.concatenate(
+        [jnp.concatenate([choose, nothing], axis=2), jnp.concatenate([nothing, choose], axis=2)], axis=0
+    )
+    choose = choose.reshape(2 * half, 2 * NZ).astype(jnp.bfloat16)
+
+    operands = [*z_forward, *x_forward, *x_back, *z_back, choose, wave_lanes, wave_kept, sums]
+    final, totals = pl.pallas_call(
+        functools.partial(travel, groups, slabs, TWO_PI / NX),
+        in_specs=[pl.BlockSpec(memory_space=pl.ANY)] + [pl.BlockSpec(memory_space=pltpu.VMEM)] * len(operands),
+        out_specs=[pl.BlockSpec(memory_space=pl.ANY)] * 2,
+        out_shape=[
+            jax.ShapeDtypeStruct((groups, rows_here, slabs, RETURNS, cols, lanes), jnp.float32),
+            jax.ShapeDtypeStruct((slabs, *sums.shape), jnp.float32),
+        ],
+        scratch_shapes=[
+            pltpu.VMEM((rows_here, devices, FIELDS, cols, lanes), jnp.float32),
+            pltpu.VMEM((rows_here, slabs, RETURNS, cols, 2 * half), jnp.float32),
+            pltpu.VMEM((rows_here, slabs, RETURNS, cols, 2 * half), jnp.float32),
+            pltpu.VMEM((rows_here, groups, slabs, RETURNS, cols, lanes), jnp.float32),
+        ]
+        + [pltpu.SemaphoreType.DMA((rows_here,))] * 8
+        + [pltpu.SemaphoreType.DMA] * 3,
+        compiler_params=pltpu.CompilerParams(vmem_limit_bytes=63 * 1024 * 1024, has_side_effects=True),
+    )(sent, *operands)
+
+    means = jnp.sum(totals, axis=(0, 2, 3)).reshape(2, groups_here).T / (GMODES * KX * NY)
     power_here = lax.dynamic_slice_in_dim(power, grp_index * groups_here, groups_here)
     damping_here = lax.dynamic_slice_in_dim(damping, grp_index * groups_here, groups_here)
     forcing = (power_here - means[:, 0]) / (2.0 * (means[:, 1] + EPSILON))
@@ -358,11 +512,10 @@
     )
     block = 8 if cols % 8 == 0 else cols
     return pl.pallas_call(
-        functools.partial(finish, slots, chunks, width),
+        functools.partial(finish, slots, 1, width),
         grid=(cols // block,),
         in_specs=[
-            pl.BlockSpec((devices, rows_chunk, RETURNS, block, lanes), lambda i: (0, 0, 0, i, 0))
-            for _ in range(chunks)
+            pl.BlockSpec((groups, rows_here, slabs, RETURNS, block, lanes), lambda i: (0, 0, 0, 0, i, 0))
         ]
         + [pl.BlockSpec((4, 2, slots, block, 128), lambda i, k=k: (0, 0, 0, i, k)) for k in range(width)]
         + [
@@ -377,7 +530,7 @@
         scratch_shapes=[pltpu.VMEM((8 * slots * block, 128), jnp.float32)] * width,
         compiler_params=params,
         cost_estimate=pl.CostEstimate(flops=1 << 33, bytes_accessed=28 << 20, transcendentals=0),
-    )(*left, *[state] * width, *y_back, zrow, xrow, yrow)
+    )(final, *[state] * width, *y_back, zrow, xrow, yrow)
 
 
 def solution(mesh):

time: 584 us -> 542 us (0.928)
  Pallas kernels: 104 us -> 527 us
  waiting for transfers between devices: 315 us -> 0 us
  blocking collectives: 111 us -> 0 us
  starting transfers between devices: 30.9 us -> 0 us
    pallas_call x5 -> x3, Pallas kernels: 104 us -> 527 us  [the longest x1 477 us: shards(): pl.pallas_call(functools.partial(travel, groups, slabs, TWO_PI / NX), in_...]
    all_to_all x4 -> x0, waiting for transfers between devices: 315 us -> none  [the longest x2 223 us: shards(): got = lax.all_to_all(sent[c], ('grp', 'slab'), 0, 0, tiled=True)]
    psum x1 -> x0, blocking collectives: 111 us -> none  [shards(): means = lax.psum(partial_value, 'slab') / (GMODES * KX * NY)]
    all_to_all x4 -> x0, starting transfers between devices: 30.9 us -> none  [the longest x2 16.4 us: shards(): left.append(lax.all_to_all(back, ('grp', 'slab'), 0, 0, tiled=True))]
    reduce_sum x4 -> x1, other arithmetic: 8.71 us -> 1.03 us  [shards(): jnp.sum(totals, axis=(0, 2, 3)).reshape(2, groups_here)]
  transfers between devices with their start and end apart: 4 -> 0, of which waited for: 3 -> 0; matrix products, arithmetic and copies ran while one was open for 3% -> 0% of each run, Pallas kernels for 10% -> 0%
where the time goes in v2:
time: 542 us
  Pallas kernels  527 us (97%)
  other arithmetic  8.34 us (2%)
    pallas_call x1, Pallas kernels, shards(): pl.pallas_call(functools.partial(travel, groups, slabs, TWO_PI / NX), in_...  477 us
    pallas_call x1, Pallas kernels, shards(): pl.pallas_call(functools.partial(forward_y, cols, slots, width, GMODES),...  26.2 us
    pallas_call x1, Pallas kernels, shards(): pl.pallas_call(functools.partial(finish, slots, 1, width), grid=(cols //...  23.8 us

profile of v2, /device:TPU:9, one launch (start us, length us, event | category | flops | bytes accessed | tf_op | source)
XLA Modules:
  0.0 542.2 jit_solution(2921781544920060727)
XLA Ops:
  0.0 3.8 sort.17
  3.8 0.1 mul.145
  3.9 1.1 fusion.10
  5.0 0.1 pad_maximum_fusion.1
  5.2 1.1 fusion
  6.3 0.1 eq.24
  6.4 0.1 iota_compare_fusion
  6.5 0.1 fusion.1
  6.6 0.9 copy.17.refs_9_
  7.6 0.1 broadcast_in_dim.16
  7.7 0.1 broadcast_in_dim.18
  7.7 0.6 broadcast_in_dim.19.refs_10_
  8.3 26.2 %shard_map.154 = (f32[32,8,6,16,128]{4,3,2,1,0:T(8,128)}, f32[4,8,128]{2,1,0:T(8,128)}) custom-call(f32[4,2,64,16,256]{4,3,2,1,0:T(8,128)} %refs_2_.3, f32[4,2,64,16,256]{4,3,2,1,0:T(8,128)} %refs_2_.3, f32[4,2,64,16,256]{4,3,2,1,0:T(8,128)} %refs_2_.3, f32[4,2,64,16,256]{4,3,2,1,0:T(8,128)} %refs_2_.3, bf16[2,512,256]{2,1,0:T(8,128)(2,1)} %constant.89.clone.refs_4_, ...), custom_call_target="tpu_custom_call" | custom-call | flops 9663676416 | bytes 20971520 | tf_op jit(solution)/shard_map/pallas_call | solution.py:418
  34.6 0.0 copy-start.1
  34.6 0.0 copy-start
  34.6 0.0 copy-start.2
  34.6 477.3 %shard_map.155 = (f32[4,8,8,5,16,128]{5,4,3,2,1,0:T(8,128)}, f32[8,4,8,128]{3,2,1,0:T(8,128)}) custom-call(f32[32,8,6,16,128]{4,3,2,1,0:T(8,128)} %get-tuple-element.10.refs_0_, bf16[512,512]{1,0:T(8,128)(2,1)} %get-tuple-element.16.refs_1_, bf16[512,512]{1,0:T(8,128)(2,1)} %get-tuple-element.15.refs_2_, bf16[2,256,256]{2,1,0:T(8,128)(2,1)} %constant.96.clone.refs_3_, ...), custom_call_target="tpu_custom_call" | custom-call | tf_op jit(solution)/shard_map/pallas_call | solution.py:464
  511.9 1.0 reduce_sum.9
  512.9 0.1 div.11
  513.0 0.0 copy-done.1
  513.0 0.1 bitcast_divide_fusion
  513.1 0.1 broadcast_in_dim.20
  513.1 0.1 stack_reshape.6
  513.2 0.0 copy-done
  513.2 0.7 fusion.12
  514.6 0.1 fusion.11
  514.7 0.1 multiply_bitcast_fusion
  514.7 0.0 copy-done.2
  514.7 0.1 dynamic_slice.11
  514.8 0.1 broadcast_in_dim.42
  514.9 0.1 stack_reshape.7
  515.0 0.8 broadcast_in_dim.43.refs_5_
  516.5 0.7 broadcast_in_dim.44.refs_6_
  517.8 0.6 pad_maximum_fusion.4.refs_7_
  518.4 23.8 %shard_map.156 = f32[4,2,64,16,256]{4,3,2,1,0:T(8,128)} custom-call(f32[4,8,8,5,16,128]{5,4,3,2,1,0:T(8,128)} %get-tuple-element.13.refs_0_, f32[4,2,64,16,256]{4,3,2,1,0:T(8,128)} %refs_2_.3, f32[4,2,64,16,256]{4,3,2,1,0:T(8,128)} %refs_2_.3, bf16[256,512]{1,0:T(8,128)(2,1)} %constant.91.clone.refs_3_, bf16[256,512]{1,0:T(8,128)(2,1)} %constant.92.clone.refs_4_, ...), custom_call_target="tpu_custom_call" | custom-call | flops 8589934592 | bytes 29360128 | tf_op jit(solution)/shard_map/pallas_call | solution.py:514
  (11 shorter events, 0.1 us)
Async XLA Ops:
  34.6 478.4 %copy-start.1 = (f32[8]{0:T(128)S(1)}, f32[8]{0:T(128)}, u32[]{:S(2)}) copy-start(f32[8]{0:T(128)} %param.20) | copy-start | bytes 100
  34.6 478.6 %copy-start = (s32[3]{0:T(128)S(1)}, s32[3]{0:T(128)}, u32[]{:S(2)}) copy-start(s32[3]{0:T(128)} %param.18) | copy-start | bytes 40
  34.6 480.2 %copy-start.2 = (f32[8]{0:T(128)S(1)}, f32[8]{0:T(128)}, u32[]{:S(2)}) copy-start(f32[8]{0:T(128)} %param.19) | copy-start | bytes 100

commit v3 on v2

--- a/solution.py
+++ b/solution.py
@@ -63,9 +63,12 @@
     high_ref, low_ref, out_ref, sums_ref = refs[2 * width :]
     out = flat_rows(out_ref)
     lanes = 2 * slots
-    count = high_ref.shape[1] // 2
+    count = high_ref.shape[0]
     rows = [flat_rows(ref) for ref in refs[:width]]
-    table = (high_ref[0], low_ref[0])
+    table = tuple(jnp.concatenate([ref[:, :count], ref[:, count:]], axis=0) for ref in (high_ref, low_ref))
+    mode = signed(lax.broadcasted_iota(jnp.int32, (1, count), 1), count).astype(jnp.float32)
+    sloped = (pl.program_id(0) == 1) | (pl.program_id(0) == 3)
+    factor = jnp.where(sloped, TWO_PI / count * mode, 1.0)
     sign = jnp.where(lax.broadcasted_iota(jnp.int32, (1, lanes), 1) < slots, -1.0, 1.0)
     pair = 2 if cols % 2 == 0 else 1
     def some(first):
@@ -74,21 +77,15 @@
             for d in range(2):
                 start = d * slots * cols + first + j
                 taken.append(jnp.concatenate([strided(part, start, slots, cols) for part in rows], axis=1))
-        data = halves(jnp.concatenate(taken, axis=0))
+        data = halves(jnp.concatenate(taken, axis=0) * factor)
         both = dot3(table, data, (((1,), (1,)), ((), ())))
         for j in range(pair):
             part = both[:, j * lanes : (j + 1) * lanes]
             result = part[:count] + sign * pltpu.roll(part[count:], slots, 1)
             out[pl.ds(first + j, count, stride=cols), :] = result
 
-    unrolled = 2 if cols % (2 * pair) == 0 else 1
-
-    def several(i, carry):
-        for k in range(unrolled):
-            some((i * unrolled + k) * pair)
-        return carry
-
-    lax.fori_loop(0, cols // (pair * unrolled), several, 0)
+    for i in range(cols // pair):
+        some(i * pair)
 
     step = pl.program_id(0)
     here = sums_ref.shape[0] // 2
@@ -148,9 +145,50 @@
         write(f, hat)
 
 
-def travel(groups, slabs, x_step, *refs):
-    (sent, zf0, zf1, xf0, xf1, xb0, xb1, zb0, zb1, choose, kz_ref, kept_ref, sums_ref, final, totals) = refs[:15]
-    (taken, made, kept, ready, f_send, f_recv, f_own, b_send, b_recv, c_send, c_recv, c_own, t_send, t_recv, t_own) = refs[15:]
+def slot_tables(members, reach, wide, group_ref, g, zf_refs, choose_ref, kz_ref, modes_ref):
+    nz = group_ref.shape[1]
+    slots = modes_ref.shape[0]
+    half = choose_ref.shape[0] // 2
+    rows = lax.broadcasted_iota(jnp.int32, (nz, nz), 0)
+    lanes = lax.broadcasted_iota(jnp.int32, (nz, nz), 1)
+    across = jnp.broadcast_to(group_ref[0:1, :], (nz, nz))
+    down = across.T
+    same = across == down
+    rank_row = jnp.sum(jnp.where(same & (rows < lanes), 1.0, 0.0), axis=0, keepdims=True)
+    rank_col = jnp.sum(jnp.where(same & (lanes < rows), 1.0, 0.0), axis=1, keepdims=True)
+    place_row = across[0:1, :] * members + rank_row
+    place_col = down[:, 0:1] * members + rank_col
+    picks = jnp.where(rows.astype(jnp.float32) == place_row, 1.0, 0.0).astype(jnp.bfloat16)
+    for part, out in zip(wide, zf_refs):
+        chosen = jnp.dot(picks, part[...], preferred_element_type=jnp.float32)
+        cosine, sine = chosen[:, :nz], chosen[:, nz:]
+        for k in range(nz // slots):
+            here = slice(k * slots, (k + 1) * slots)
+            start = 2 * k * slots
+            out[start : start + slots, :nz] = cosine[here].astype(jnp.bfloat16)
+            out[start : start + slots, nz:] = sine[here].astype(jnp.bfloat16)
+            out[start + slots : start + 2 * slots, :nz] = (-sine[here]).astype(jnp.bfloat16)
+            out[start + slots : start + 2 * slots, nz:] = cosine[here].astype(jnp.bfloat16)
+    lane = lax.broadcasted_iota(jnp.int32, (1, 2 * nz), 1)
+    slot = (lane // (2 * slots) * slots + lane % slots).astype(jnp.float32)
+    mode_col = signed(lax.broadcasted_iota(jnp.int32, (nz, 1), 0), nz).astype(jnp.float32)
+    mode = jnp.sum(jnp.where(place_col == slot, mode_col, 0.0), axis=0, keepdims=True)
+    kz_ref[...] = jnp.broadcast_to(TWO_PI / nz * mode, kz_ref.shape)
+    part = (lane % (2 * slots) >= slots).astype(jnp.int32)
+    row = lax.broadcasted_iota(jnp.int32, (half, 1), 0)
+    hit = jnp.where((row - reach).astype(jnp.float32) == mode, 1.0, 0.0)
+    for d in range(2):
+        choose_ref[d * half : (d + 1) * half, :] = jnp.where(part == d, hit, 0.0).astype(jnp.bfloat16)
+    mine = (lax.broadcasted_iota(jnp.int32, (slots, 1), 0) + g * slots).astype(jnp.float32)
+    mode_row = signed(lax.broadcasted_iota(jnp.int32, (1, nz), 1), nz).astype(jnp.float32)
+    own = jnp.sum(jnp.where(place_row == mine, mode_row, 0.0), axis=1, keepdims=True)
+    modes_ref[...] = jnp.broadcast_to(own, modes_ref.shape)
+
+
+def travel(groups, slabs, x_step, members, reach, *refs):
+    (sent, wide0, wide1, xf0, xf1, xb0, xb1, zb0, zb1, group_ref, kept_ref, sums_ref, final, totals, modes) = refs[:15]
+    zf0, zf1, choose, kz_ref = refs[15:19]
+    (taken, made, kept, ready, f_send, f_recv, f_own, b_send, b_recv, c_send, c_recv, c_own, t_send, t_recv, t_own) = refs[19:]
     devices = groups * slabs
     count = taken.shape[0]
     cols, lanes = taken.shape[3:]
@@ -195,13 +233,13 @@
         lax.fori_loop(1, slabs, one, 0)
 
     def own_c(y):
-        return pltpu.make_async_copy(ready.at[y, g], final.at[g, y], c_own.at[y])
+        return pltpu.make_async_copy(ready.at[y, g], final.at[g, :, y], c_own.at[y])
 
     def send_c(y):
         own_c(y).start()
         for k in range(1, groups):
             to = lax.rem(g + k, groups)
-            remote(ready.at[y, to], final.at[g, y], c_send.at[y], c_recv.at[y], to, s)
+            remote(ready.at[y, to], final.at[g, :, y], c_send.at[y], c_recv.at[y], to, s)
 
     own_t = pltpu.make_async_copy(sums_ref, totals.at[s], t_own)
 
@@ -217,6 +255,7 @@
         return carry
 
     lax.fori_loop(1, slabs, send_t, 0)
+    slot_tables(members, reach, (wide0, wide1), group_ref, g, (zf0, zf1), choose, kz_ref, modes)
 
     def step(t, carry):
         @pl.when(t < count)
@@ -266,7 +305,7 @@
 
     def last(y, carry):
         own_c(y).wait()
-        wait_all(final.at[pl.ds(0, groups - 1), y], c_recv.at[y])
+        wait_all(final.at[pl.ds(0, groups - 1), :, y], c_recv.at[y])
         wait_all(taken.at[y, pl.ds(0, devices - 1)], f_send.at[y])
         wait_all(kept.at[y, pl.ds(0, slabs - 1)], b_send.at[y])
         wait_all(ready.at[y, pl.ds(0, groups - 1)], c_send.at[y])
@@ -278,18 +317,42 @@
     wait_all(totals.at[pl.ds(0, slabs - 1)], t_send)
 
 
-def finish(slots, chunks, width, *refs):
-    in_refs = refs[:chunks]
-    state_refs = refs[chunks : chunks + width]
-    high_ref, low_ref, zrow_ref, xrow_ref, yrow_ref, out_ref = refs[chunks + width : chunks + width + 6]
-    out_parts = refs[chunks + width + 6 :]
+def finish(slots, width, sizes, members, *refs):
+    nx, ny, nz = sizes
+    state_refs = refs[1 : width + 1]
+    high_ref, low_ref, modes_ref, totals_ref, cutoffs_ref, damping_ref, power_ref, out_ref = refs[width + 1 : width + 9]
+    out_parts = refs[width + 9 :]
     block = out_ref.shape[3]
-    ny = out_ref.shape[4]
-    inputs = [flat_rows(ref) for ref in in_refs]
+    rows = flat_rows(refs[0])
     state = [flat_rows(ref) for ref in state_refs]
     table = (high_ref[...], low_ref[...])
-    wave_z, kept_z, forcing, damping = (zrow_ref[k] for k in range(4))
-    wave_y, kept_y = yrow_ref[0:1, :], yrow_ref[1:2, :]
+    here = slots // members
+    first_group = lax.axis_index("grp") * here
+    x_count = pl.num_programs(0) * block
+    first_x = lax.axis_index("slab") * x_count + pl.program_id(0) * block
+    cells = members * (nx // 2) * ny
+    sums = jnp.sum(totals_ref[...], axis=0)
+    growths, dampings = [], []
+    for group in range(here):
+        flux, energy = (
+            jnp.sum(jnp.sum(sums[k], axis=0, keepdims=True), axis=1, keepdims=True) / cells
+            for k in (group, here + group)
+        )
+        forcing = (power_ref[first_group + group] - flux) / (2.0 * (energy + EPSILON))
+        growths.append(jnp.broadcast_to(1.0 + TIME_STEP * forcing, (members, ny)))
+        dampings.append(jnp.full((members, ny), damping_ref[first_group + group], jnp.float32))
+    growth = jnp.concatenate(growths, axis=0)
+    damping = jnp.concatenate(dampings, axis=0)
+    mode_z = jnp.concatenate([modes_ref[...]] * width, axis=1)
+    wave_z = TWO_PI / nz * mode_z
+    mode_y = signed(lax.broadcasted_iota(jnp.int32, (1, ny), 1), ny).astype(jnp.float32)
+    wave_y = TWO_PI / ny * mode_y
+
+    def within(mode, which, length):
+        limit = (cutoffs_ref[which] * length).astype(jnp.float32)
+        return jnp.where(96.0 * jnp.abs(mode) <= limit, 1.0, 0.0)
+
+    kept_yz = within(mode_z, 2, nz) * within(mode_y, 1, ny) * TIME_STEP
 
     def load(c, d, x):
         start = (c * 2 + d) * slots * block + x
@@ -300,30 +363,23 @@
         for k in range(width):
             out_parts[k][pl.ds(start, slots, stride=block), :] = value[:, 128 * k : 128 * (k + 1)]
 
-    def one(x, carry):
-        columns = []
-        for f in range(RETURNS):
-            pieces = []
-            for rows in inputs:
-                count = rows.shape[0] // (RETURNS * block)
-                pieces.append(rows[pl.ds(f * block + x, count, stride=RETURNS * block), :])
-            columns.append(jnp.concatenate(pieces, axis=0).T)
+    def one(x):
+        columns = [rows[pl.ds(f * block + x, ny, stride=RETURNS * block), :].T for f in range(RETURNS)]
         both = dot3(halves(jnp.concatenate(columns, axis=0)), table)
         tends = []
         for f in range(RETURNS):
             re = both[2 * f * slots : (2 * f + 1) * slots]
             im = both[(2 * f + 1) * slots : (2 * f + 2) * slots]
             tends.append((re[:, :ny] + im[:, ny:], im[:, :ny] - re[:, ny:]))
-        wave_x = xrow_ref[0, pl.ds(x, 1), :]
-        kept = (kept_z * kept_y) * xrow_ref[1, pl.ds(x, 1), :]
-        kept = kept * TIME_STEP
+        mode_x = jnp.full((1, ny), (first_x + x).astype(jnp.float32), jnp.float32)
+        wave_x = TWO_PI / nx * mode_x
+        kept = kept_yz * within(mode_x, 0, nx)
         wave_sq = wave_x * wave_x + wave_y * wave_y + wave_z * wave_z
         implicit = 1.0 + TIME_STEP * damping * wave_sq
         rotation = TIME_STEP * CORIOLIS
         first = 1.0 / (implicit * implicit + rotation * rotation)
         second = 1.0 / (implicit * implicit + TIME_STEP * TIME_STEP * BRUNT_SQUARED)
         inverse_sq = 1.0 / (wave_sq + (wave_sq == 0).astype(jnp.float32))
-        growth = 1.0 + TIME_STEP * forcing
         total = [tends[3][d] + wave_y * tends[4][d] for d in range(2)]
         source = [total[1], -total[0]]
         for d in range(2):
@@ -340,9 +396,15 @@
             store(1, d, x, new_y - wave_y * inner)
             store(2, d, x, new_z - wave_z * inner)
             store(3, d, x, new_b)
+
+    unrolled = 2 if block % 2 == 0 else 1
+
+    def some(i, carry):
+        for k in range(unrolled):
+            one(i * unrolled + k)
         return carry
 
-    lax.fori_loop(0, block, one, 0)
+    lax.fori_loop(0, block // unrolled, some, 0)
     for k in range(width):
         for c in range(4):
             for d in range(2):
@@ -358,8 +420,6 @@
 def shards(state, kz_group, cutoffs, damping, power):
     groups = lax.axis_size("grp")
     slabs = lax.axis_size("slab")
-    grp_index = lax.axis_index("grp")
-    slab_index = lax.axis_index("slab")
     slots = state.shape[2]
     cols = state.shape[3]
     NY = state.shape[4]
@@ -375,13 +435,10 @@
     width = NY // 128
     normalizer = 1.0 / math.sqrt(NX * NY * NZ)
 
-    mode_y = np.fft.fftfreq(NY, 1.0 / NY).astype(np.int64)
-    cos_y, sin_y = trig(np.arange(NY), np.arange(NY), NY)
-    wave_np = TWO_PI / NY * mode_y
-    plain = np.concatenate([cos_y, sin_y], axis=0)
-    y_forward = constant_halves(np.stack([plain, plain * wave_np]))
-    order = np.arange(NY).reshape(groups, slabs, rows_here).transpose(0, 2, 1).reshape(-1)
-    y_back = constant_halves(np.concatenate([cos_y, sin_y], axis=1)[order])
+    wide_y = constant_halves(np.concatenate(trig(np.arange(NY), np.arange(NY), NY), axis=1))
+    wide_z = wide_y
+    if NZ != NY:
+        wide_z = constant_halves(np.concatenate(trig(np.arange(NZ), np.arange(NZ), NZ), axis=1))
     reach = WIDEST * NZ // 96
     half = -(-(2 * reach + 1) // 64) * 64
     mode_kept = np.arange(half) - reach
@@ -420,7 +477,7 @@
         grid=(FIELDS,),
         in_specs=state_step
         + state_w
-        + [pl.BlockSpec((1, 2 * NY, NY), lambda i: (jnp.where(i < 4, i % 2, 0), 0, 0))] * 2,
+        + [whole(part) for part in wide_y],
         out_specs=[
             pl.BlockSpec((devices, rows_here, 1, cols, lanes), lambda i: (0, 0, i, 0, 0)),
             pl.BlockSpec((2 * groups_here, 8, 128), lambda i: (0, 0, 0)),
@@ -433,43 +490,24 @@
         cost_estimate=pl.CostEstimate(
             flops=2 * 3 * FIELDS * 2 * NY * NY * cols * lanes, bytes_accessed=20 << 20, transcendentals=0
         ),
-    )(*[state] * (2 * width), *y_forward)
-
-    slot_mode = jnp.argsort(kz_group, stable=True).astype(jnp.int32)
-    phase = slot_mode[:, None] * jnp.arange(NZ, dtype=jnp.int32)[None, :] % NZ
-    theta = phase.astype(jnp.float32) * (TWO_PI / NZ)
-    cos_z = jnp.cos(theta).reshape(groups, 1, slots, NZ)
-    sin_z = jnp.sin(theta).reshape(groups, 1, slots, NZ)
-    z_real = jnp.concatenate([cos_z, -sin_z], axis=1).reshape(2 * NZ, NZ)
-    z_imag = jnp.concatenate([sin_z, cos_z], axis=1).reshape(2 * NZ, NZ)
-    z_table = jnp.concatenate([z_real, z_imag], axis=1)
-    z_high = lax.reduce_precision(z_table, 8, 7)
-    z_low = (z_table - z_high).astype(jnp.bfloat16)
-    z_high = z_high.astype(jnp.bfloat16)
-    z_forward = (z_high, z_low)
-    wave_slot = signed(slot_mode, NZ)
-    wave_all = TWO_PI / NZ * wave_slot.astype(jnp.float32)
-    wave_lanes = jnp.broadcast_to(wave_all.reshape(groups, 1, slots), (groups, 2, slots)).reshape(1, 2 * NZ)
-    wave_lanes = jnp.broadcast_to(wave_lanes, (8, 2 * NZ))
-
-    place = wave_slot + reach
-    choose = (place[None, :] == jnp.arange(half, dtype=jnp.int32)[:, None]).reshape(half, groups, 1, slots)
-    nothing = jnp.zeros_like(choose)
-    choose = jnp.concatenate(
-        [jnp.concatenate([choose, nothing], axis=2), jnp.concatenate([nothing, choose], axis=2)], axis=0
-    )
-    choose = choose.reshape(2 * half, 2 * NZ).astype(jnp.bfloat16)
-
-    operands = [*z_forward, *x_forward, *x_back, *z_back, choose, wave_lanes, wave_kept, sums]
-    final, totals = pl.pallas_call(
-        functools.partial(travel, groups, slabs, TWO_PI / NX),
+    )(*[state] * (2 * width), *wide_y)
+
+    group_row = jnp.broadcast_to(kz_group[None, :].astype(jnp.float32), (8, NZ))
+    operands = [*wide_z, *x_forward, *x_back, *z_back, group_row, wave_kept, sums]
+    final, totals, modes = pl.pallas_call(
+        functools.partial(travel, groups, slabs, TWO_PI / NX, GMODES, reach),
         in_specs=[pl.BlockSpec(memory_space=pl.ANY)] + [pl.BlockSpec(memory_space=pltpu.VMEM)] * len(operands),
-        out_specs=[pl.BlockSpec(memory_space=pl.ANY)] * 2,
+        out_specs=[pl.BlockSpec(memory_space=pl.ANY)] * 2 + [pl.BlockSpec(memory_space=pltpu.VMEM)],
         out_shape=[
-            jax.ShapeDtypeStruct((groups, rows_here, slabs, RETURNS, cols, lanes), jnp.float32),
+            jax.ShapeDtypeStruct((groups, slabs, rows_here, RETURNS, cols, lanes), jnp.float32),
             jax.ShapeDtypeStruct((slabs, *sums.shape), jnp.float32),
+            jax.ShapeDtypeStruct((slots, 128), jnp.float32),
         ],
         scratch_shapes=[
+            pltpu.VMEM((2 * NZ, 2 * NZ), jnp.bfloat16),
+            pltpu.VMEM((2 * NZ, 2 * NZ), jnp.bfloat16),
+            pltpu.VMEM((2 * half, 2 * NZ), jnp.bfloat16),
+            pltpu.VMEM((8, 2 * NZ), jnp.float32),
             pltpu.VMEM((rows_here, devices, FIELDS, cols, lanes), jnp.float32),
             pltpu.VMEM((rows_here, slabs, RETURNS, cols, 2 * half), jnp.float32),
             pltpu.VMEM((rows_here, slabs, RETURNS, cols, 2 * half), jnp.float32),
@@ -480,57 +518,20 @@
         compiler_params=pltpu.CompilerParams(vmem_limit_bytes=63 * 1024 * 1024, has_side_effects=True),
     )(sent, *operands)
 
-    means = jnp.sum(totals, axis=(0, 2, 3)).reshape(2, groups_here).T / (GMODES * KX * NY)
-    power_here = lax.dynamic_slice_in_dim(power, grp_index * groups_here, groups_here)
-    damping_here = lax.dynamic_slice_in_dim(damping, grp_index * groups_here, groups_here)
-    forcing = (power_here - means[:, 0]) / (2.0 * (means[:, 1] + EPSILON))
-
-    local_mode = signed(lax.dynamic_slice_in_dim(slot_mode, grp_index * slots, slots), NZ)
-    mode_x = slab_index * cols + jnp.arange(cols, dtype=jnp.int32)
-    mode_y = signed(jnp.arange(NY, dtype=jnp.int32), NY)
-    zrow = jnp.stack(
-        [
-            TWO_PI / NZ * local_mode.astype(jnp.float32),
-            (96 * jnp.abs(local_mode) <= cutoffs[2] * NZ).astype(jnp.float32),
-            jnp.repeat(forcing, GMODES),
-            jnp.repeat(damping_here, GMODES),
-        ]
-    )
-    zrow = jnp.broadcast_to(zrow[:, :, None], (4, slots, NY))
-    xrow = jnp.stack(
-        [
-            TWO_PI / NX * mode_x.astype(jnp.float32),
-            (96 * mode_x <= cutoffs[0] * NX).astype(jnp.float32),
-        ]
-    )
-    xrow = jnp.broadcast_to(xrow[:, :, None], (2, cols, NY))
-    yrow = jnp.stack(
-        [
-            TWO_PI / NY * mode_y.astype(jnp.float32),
-            (96 * jnp.abs(mode_y) <= cutoffs[1] * NY).astype(jnp.float32),
-        ]
-    )
     block = 8 if cols % 8 == 0 else cols
     return pl.pallas_call(
-        functools.partial(finish, slots, 1, width),
+        functools.partial(finish, slots, width, (NX, NY, NZ), GMODES),
         grid=(cols // block,),
-        in_specs=[
-            pl.BlockSpec((groups, rows_here, slabs, RETURNS, block, lanes), lambda i: (0, 0, 0, 0, i, 0))
-        ]
+        in_specs=[pl.BlockSpec((groups, slabs, rows_here, RETURNS, block, lanes), lambda i: (0, 0, 0, 0, i, 0))]
         + [pl.BlockSpec((4, 2, slots, block, 128), lambda i, k=k: (0, 0, 0, i, k)) for k in range(width)]
-        + [
-            whole(y_back[0]),
-            whole(y_back[1]),
-            whole(zrow),
-            pl.BlockSpec((2, block, NY), lambda i: (0, i, 0)),
-            whole(yrow),
-        ],
+        + [whole(wide_y[0]), whole(wide_y[1]), whole(modes), whole(totals)]
+        + [pl.BlockSpec(memory_space=pltpu.SMEM)] * 3,
         out_specs=pl.BlockSpec((4, 2, slots, block, NY), lambda i: (0, 0, 0, i, 0)),
         out_shape=jax.ShapeDtypeStruct(state.shape, jnp.float32),
         scratch_shapes=[pltpu.VMEM((8 * slots * block, 128), jnp.float32)] * width,
         compiler_params=params,
         cost_estimate=pl.CostEstimate(flops=1 << 33, bytes_accessed=28 << 20, transcendentals=0),
-    )(final, *[state] * width, *y_back, zrow, xrow, yrow)
+    )(final, *[state] * width, *wide_y, modes, totals, cutoffs, damping, power)
 
 
 def solution(mesh):

time: 542 us -> 522 us (0.963)
  other arithmetic: 8.34 us -> 0.68 us
  Pallas kernels: 527 us -> 521 us
    pallas_call x1, Pallas kernels: 26.2 us -> 19.7 us  [shards(): pl.pallas_call(functools.partial(forward_y, cols, slots, width, GMODES),...]
where the time goes in v3:
time: 522 us
  Pallas kernels  521 us (100%)
    pallas_call x1, Pallas kernels, shards(): pl.pallas_call(functools.partial(travel, groups, slabs, TWO_PI / NX, GMOD...  478 us
    pallas_call x1, Pallas kernels, shards(): pl.pallas_call(functools.partial(finish, slots, width, (NX, NY, NZ), GMOD...  23.3 us
    pallas_call x1, Pallas kernels, shards(): pl.pallas_call(functools.partial(forward_y, cols, slots, width, GMODES),...  19.7 us

profile of v3, /device:TPU:9, one launch (start us, length us, event | category | flops | bytes accessed | tf_op | source)
XLA Modules:
  0.0 522.0 jit_solution(12543090859531107396)
XLA Ops:
  0.0 0.7 convert_element_type.4
  0.7 0.6 broadcast_in_dim.2.refs_9_
  1.3 19.7 %shard_map.136 = (f32[32,8,6,16,128]{4,3,2,1,0:T(8,128)}, f32[4,8,128]{2,1,0:T(8,128)}) custom-call(f32[4,2,64,16,256]{4,3,2,1,0:T(8,128)} %refs_2_.4, f32[4,2,64,16,256]{4,3,2,1,0:T(8,128)} %refs_2_.4, f32[4,2,64,16,256]{4,3,2,1,0:T(8,128)} %refs_2_.4, f32[4,2,64,16,256]{4,3,2,1,0:T(8,128)} %refs_2_.4, ...), custom_call_target="tpu_custom_call" | custom-call | flops 9663676416 | bytes 20971520 | tf_op jit(solution)/shard_map/pallas_call | solution.py:475
  21.0 477.6 %shard_map.137 = (f32[4,8,8,5,16,128]{5,4,3,2,1,0:T(8,128)}, f32[8,4,8,128]{3,2,1,0:T(8,128)}, f32[64,128]{1,0:T(8,128)}) custom-call(f32[32,8,6,16,128]{4,3,2,1,0:T(8,128)} %get-tuple-element.10.refs_0_, bf16[256,512]{1,0:T(8,128)(2,1)} %constant.18.clone.refs_4_.refs_1_.refs_3_, bf16[256,512]{1,0:T(8,128)(2,1)} %constant.19.clone.refs_5_.refs_2_.refs_4_, ...), custom_call_target="tpu_custom_call" | custom-call | tf_op jit(solution)/shard_map/pallas_call | solution.py:497
  498.6 23.3 %shard_map.138 = f32[4,2,64,16,256]{4,3,2,1,0:T(8,128)} custom-call(f32[4,8,8,5,16,128]{5,4,3,2,1,0:T(8,128)} %get-tuple-element.12.refs_0_, f32[4,2,64,16,256]{4,3,2,1,0:T(8,128)} %refs_2_.4, f32[4,2,64,16,256]{4,3,2,1,0:T(8,128)} %refs_2_.4, bf16[256,512]{1,0:T(8,128)(2,1)} %constant.18.clone.refs_4_.refs_1_.refs_3_, ...), custom_call_target="tpu_custom_call" | custom-call | flops 8589934592 | bytes 29360128 | tf_op jit(solution)/shard_map/pallas_call | solution.py:522

commit v4 on v3

--- a/solution.py
+++ b/solution.py
@@ -16,6 +16,7 @@
 EPSILON = 1e-06
 AHEAD = 3
 LAG = 3
+PARTS = ((0, 3), (3, 5))
 WIDEST = 32
 FIELDS = 6
 RETURNS = 5
@@ -224,22 +225,43 @@
 
         lax.fori_loop(1, devices, one, 0)
 
+    parts = len(PARTS)
+
     def send_b(y):
-        def one(k, carry):
-            to = lax.rem(s + k, slabs)
-            remote(made.at[y, to], kept.at[y, s], b_send.at[y], b_recv.at[y], g, to)
-            return carry
-
-        lax.fori_loop(1, slabs, one, 0)
-
-    def own_c(y):
-        return pltpu.make_async_copy(ready.at[y, g], final.at[g, :, y], c_own.at[y])
-
-    def send_c(y):
-        own_c(y).start()
+        for p, (low, high) in enumerate(PARTS):
+            fields = pl.ds(low, high - low)
+
+            def one(k, carry):
+                to = lax.rem(s + k, slabs)
+                q = y * parts + p
+                remote(made.at[y, to, fields], kept.at[y, s, fields], b_send.at[q], b_recv.at[q], g, to)
+                return carry
+
+            lax.fori_loop(1, slabs, one, 0)
+
+    def own_c(y, p):
+        fields = pl.ds(PARTS[p][0], PARTS[p][1] - PARTS[p][0])
+        return pltpu.make_async_copy(ready.at[y, g, :, fields], final.at[g, :, y, fields], c_own.at[y * parts + p])
+
+    def send_c(y, p):
+        own_c(y, p).start()
+        fields = pl.ds(PARTS[p][0], PARTS[p][1] - PARTS[p][0])
+        q = y * parts + p
         for k in range(1, groups):
             to = lax.rem(g + k, groups)
-            remote(ready.at[y, to], final.at[g, :, y], c_send.at[y], c_recv.at[y], to, s)
+            remote(ready.at[y, to, :, fields], final.at[g, :, y, fields], c_send.at[q], c_recv.at[q], to, s)
+
+    def back(y, p):
+        low, high = PARTS[p]
+        size = high - low
+        wait_all(kept.at[y, pl.ds(0, slabs - 1), pl.ds(low, size)], b_recv.at[y * parts + p])
+        data = kept[y, :, low:high]
+        upper, lower = halves(data.reshape(slabs * size * cols, data.shape[-1]))
+        dot = functools.partial(jnp.dot, preferred_element_type=jnp.float32)
+        picked = dot(upper, choose[...]) + dot(lower, choose[...])
+        for group in range(groups):
+            part = picked[:, group * lanes : (group + 1) * lanes]
+            ready[y, group, :, low:high] = part.reshape(slabs, size, cols, lanes)
 
     own_t = pltpu.make_async_copy(sums_ref, totals.at[s], t_own)
 
@@ -281,15 +303,7 @@
 
         @pl.when(t >= lag)
         def _():
-            y = t - lag
-            wait_all(kept.at[y, pl.ds(0, slabs - 1)], b_recv.at[y])
-            data = kept[y]
-            high, low = halves(data.reshape(slabs * RETURNS * cols, data.shape[-1]))
-            dot = functools.partial(jnp.dot, preferred_element_type=jnp.float32)
-            picked = dot(high, choose[...]) + dot(low, choose[...])
-            for group in range(groups):
-                part = picked[:, group * lanes : (group + 1) * lanes]
-                ready[y, group] = part.reshape(slabs, RETURNS, cols, lanes)
+            back(t - lag, 0)
 
         @pl.when(t < count)
         def _():
@@ -297,18 +311,24 @@
 
         @pl.when(t >= lag)
         def _():
-            send_c(t - lag)
+            send_c(t - lag, 0)
+            for p in range(1, parts):
+                back(t - lag, p)
+                send_c(t - lag, p)
 
         return carry
 
     lax.fori_loop(0, count + lag, step, 0)
 
     def last(y, carry):
-        own_c(y).wait()
-        wait_all(final.at[pl.ds(0, groups - 1), :, y], c_recv.at[y])
         wait_all(taken.at[y, pl.ds(0, devices - 1)], f_send.at[y])
-        wait_all(kept.at[y, pl.ds(0, slabs - 1)], b_send.at[y])
-        wait_all(ready.at[y, pl.ds(0, groups - 1)], c_send.at[y])
+        for p, (low, high) in enumerate(PARTS):
+            fields = pl.ds(low, high - low)
+            q = y * parts + p
+            own_c(y, p).wait()
+            wait_all(final.at[pl.ds(0, groups - 1), :, y, fields], c_recv.at[q])
+            wait_all(kept.at[y, pl.ds(0, slabs - 1), fields], b_send.at[q])
+            wait_all(ready.at[y, pl.ds(0, groups - 1), :, fields], c_send.at[q])
         return carry
 
     lax.fori_loop(0, count, last, 0)
@@ -397,7 +417,7 @@
             store(2, d, x, new_z - wave_z * inner)
             store(3, d, x, new_b)
 
-    unrolled = 2 if block % 2 == 0 else 1
+    unrolled = 4 if block % 4 == 0 else 1
 
     def some(i, carry):
         for k in range(unrolled):
@@ -513,7 +533,8 @@
             pltpu.VMEM((rows_here, slabs, RETURNS, cols, 2 * half), jnp.float32),
             pltpu.VMEM((rows_here, groups, slabs, RETURNS, cols, lanes), jnp.float32),
         ]
-        + [pltpu.SemaphoreType.DMA((rows_here,))] * 8
+        + [pltpu.SemaphoreType.DMA((rows_here,))] * 3
+        + [pltpu.SemaphoreType.DMA((rows_here * len(PARTS),))] * 5
         + [pltpu.SemaphoreType.DMA] * 3,
         compiler_params=pltpu.CompilerParams(vmem_limit_bytes=63 * 1024 * 1024, has_side_effects=True),
     )(sent, *operands)

time: 522 us -> 517 us (level)
  no operation moved by 1% of the time
where the time goes in v4:
time: 517 us
  Pallas kernels  516 us (100%)
    pallas_call x1, Pallas kernels, shards(): pl.pallas_call(functools.partial(travel, groups, slabs, TWO_PI / NX, GMOD...  474 us
    pallas_call x1, Pallas kernels, shards(): pl.pallas_call(functools.partial(finish, slots, width, (NX, NY, NZ), GMOD...  22.2 us
    pallas_call x1, Pallas kernels, shards(): pl.pallas_call(functools.partial(forward_y, cols, slots, width, GMODES),...  19.7 us

profile of v4, /device:TPU:9, one launch (start us, length us, event | category | flops | bytes accessed | tf_op | source)
XLA Modules:
  0.0 517.0 jit_solution(14184677689621118936)
XLA Ops:
  0.0 0.7 convert_element_type.4
  0.7 0.6 broadcast_in_dim.2.refs_9_
  1.3 19.7 %shard_map.136 = (f32[32,8,6,16,128]{4,3,2,1,0:T(8,128)}, f32[4,8,128]{2,1,0:T(8,128)}) custom-call(f32[4,2,64,16,256]{4,3,2,1,0:T(8,128)} %refs_2_.4, f32[4,2,64,16,256]{4,3,2,1,0:T(8,128)} %refs_2_.4, f32[4,2,64,16,256]{4,3,2,1,0:T(8,128)} %refs_2_.4, f32[4,2,64,16,256]{4,3,2,1,0:T(8,128)} %refs_2_.4, ...), custom_call_target="tpu_custom_call" | custom-call | flops 9663676416 | bytes 20971520 | tf_op jit(solution)/shard_map/pallas_call | solution.py:495
  21.0 473.8 %shard_map.137 = (f32[4,8,8,5,16,128]{5,4,3,2,1,0:T(8,128)}, f32[8,4,8,128]{3,2,1,0:T(8,128)}, f32[64,128]{1,0:T(8,128)}) custom-call(f32[32,8,6,16,128]{4,3,2,1,0:T(8,128)} %get-tuple-element.10.refs_0_, bf16[256,512]{1,0:T(8,128)(2,1)} %constant.18.clone.refs_4_.refs_1_.refs_3_, bf16[256,512]{1,0:T(8,128)(2,1)} %constant.19.clone.refs_5_.refs_2_.refs_4_, ...), custom_call_target="tpu_custom_call" | custom-call | tf_op jit(solution)/shard_map/pallas_call | solution.py:517
  494.8 22.2 %shard_map.138 = f32[4,2,64,16,256]{4,3,2,1,0:T(8,128)} custom-call(f32[4,8,8,5,16,128]{5,4,3,2,1,0:T(8,128)} %get-tuple-element.12.refs_0_, f32[4,2,64,16,256]{4,3,2,1,0:T(8,128)} %refs_2_.4, f32[4,2,64,16,256]{4,3,2,1,0:T(8,128)} %refs_2_.4, bf16[256,512]{1,0:T(8,128)(2,1)} %constant.18.clone.refs_4_.refs_1_.refs_3_, ...), custom_call_target="tpu_custom_call" | custom-call | flops 8589934592 | bytes 29360128 | tf_op jit(solution)/shard_map/pallas_call | solution.py:543

commit v5 on v4

--- a/solution.py
+++ b/solution.py
@@ -16,7 +16,7 @@
 EPSILON = 1e-06
 AHEAD = 3
 LAG = 3
-PARTS = ((0, 3), (3, 5))
+PARTS = ((0, 2), (2, 4), (4, 5))
 WIDEST = 32
 FIELDS = 6
 RETURNS = 5

time: 517 us -> 515 us (level)
  no operation moved by 1% of the time
where the time goes in v5:
time: 515 us
  Pallas kernels  514 us (100%)
    pallas_call x1, Pallas kernels, shards(): pl.pallas_call(functools.partial(travel, groups, slabs, TWO_PI / NX, GMOD...  472 us
    pallas_call x1, Pallas kernels, shards(): pl.pallas_call(functools.partial(finish, slots, width, (NX, NY, NZ), GMOD...  22.2 us
    pallas_call x1, Pallas kernels, shards(): pl.pallas_call(functools.partial(forward_y, cols, slots, width, GMODES),...  19.7 us

profile of v5, /device:TPU:9, one launch (start us, length us, event | category | flops | bytes accessed | tf_op | source)
XLA Modules:
  0.0 515.1 jit_solution(34593963662556218)
XLA Ops:
  0.0 0.7 convert_element_type.4
  0.7 0.6 broadcast_in_dim.2.refs_9_
  1.3 19.7 %shard_map.136 = (f32[32,8,6,16,128]{4,3,2,1,0:T(8,128)}, f32[4,8,128]{2,1,0:T(8,128)}) custom-call(f32[4,2,64,16,256]{4,3,2,1,0:T(8,128)} %refs_2_.4, f32[4,2,64,16,256]{4,3,2,1,0:T(8,128)} %refs_2_.4, f32[4,2,64,16,256]{4,3,2,1,0:T(8,128)} %refs_2_.4, f32[4,2,64,16,256]{4,3,2,1,0:T(8,128)} %refs_2_.4, ...), custom_call_target="tpu_custom_call" | custom-call | flops 9663676416 | bytes 20971520 | tf_op jit(solution)/shard_map/pallas_call | solution.py:495
  21.0 471.9 %shard_map.137 = (f32[4,8,8,5,16,128]{5,4,3,2,1,0:T(8,128)}, f32[8,4,8,128]{3,2,1,0:T(8,128)}, f32[64,128]{1,0:T(8,128)}) custom-call(f32[32,8,6,16,128]{4,3,2,1,0:T(8,128)} %get-tuple-element.10.refs_0_, bf16[256,512]{1,0:T(8,128)(2,1)} %constant.18.clone.refs_4_.refs_1_.refs_3_, bf16[256,512]{1,0:T(8,128)(2,1)} %constant.19.clone.refs_5_.refs_2_.refs_4_, ...), custom_call_target="tpu_custom_call" | custom-call | tf_op jit(solution)/shard_map/pallas_call | solution.py:517
  492.9 22.2 %shard_map.138 = f32[4,2,64,16,256]{4,3,2,1,0:T(8,128)} custom-call(f32[4,8,8,5,16,128]{5,4,3,2,1,0:T(8,128)} %get-tuple-element.12.refs_0_, f32[4,2,64,16,256]{4,3,2,1,0:T(8,128)} %refs_2_.4, f32[4,2,64,16,256]{4,3,2,1,0:T(8,128)} %refs_2_.4, bf16[256,512]{1,0:T(8,128)(2,1)} %constant.18.clone.refs_4_.refs_1_.refs_3_, ...), custom_call_target="tpu_custom_call" | custom-call | flops 8589934592 | bytes 29360128 | tf_op jit(solution)/shard_map/pallas_call | solution.py:543
